TPU v7x, 32 devices: a whole 2x2x4 slice. The times are simulated.
32 devices in a mesh: gx: 4 (over x, core), gy: 2 (over y), gz: 4 (over z).
Axes of the slice: x: 2, y: 2, z: 4, core: 2. Of those that a mesh axis runs over, the one named last changes fastest.
Arguments:
- solution: float32 [16, 8, 16, 256], P(None, 'gx', 'gz', 'gy'), may hold values from -0.6 to 0.6
- residual: float32 [16, 8, 16, 256], P(None, 'gx', 'gz', 'gy'), may hold values from -6 to 6
- direction_prev: float32 [16, 8, 16, 256], P(None, 'gx', 'gz', 'gy'), may hold values from -0.3 to 0.3, as said below
- image_prev: float32 [16, 8, 16, 256], P(None, 'gx', 'gz', 'gy'), may hold values from -9 to 9, as said below
- gram_prev: float32 [16, 16], replicated, may hold values from -32768 to 32768, as said below
Outputs:
- solution_new: float32 [16, 8, 16, 256], P(None, 'gx', 'gz', 'gy')
- residual_new: float32 [16, 8, 16, 256], P(None, 'gx', 'gz', 'gy')
- direction: float32 [16, 8, 16, 256], P(None, 'gx', 'gz', 'gy')
Inputs may be any that keep to these rules, and one draw needn't show every extreme that they name: direction_prev is a field of order 0.05. image_prev equals A direction_prev, computed in float32. gram_prev is symmetric and positive definite.
All inputs are finite; a program needn't handle non-finite values.
Results may differ from a plain program's by a relative error of at most 0.0001.
Values sent between devices are 32-bit elements; how exact they have to be, the bound alone decides.
A program may use at most 64 MiB of HBM per device.

v0:
```python
import jax
import jax.numpy as jnp
from jax import lax
from jax.sharding import PartitionSpec as P


def with_halo(value, sides, width):
    for axis, dim in sides:
        devices, length = (lax.axis_size(axis), value.shape[dim])
        up = [(i, (i + 1) % devices) for i in range(devices - 1)]
        down = [(j, i) for i, j in up]
        last = lax.slice_in_dim(value, length - width, length, axis=dim)
        first = lax.slice_in_dim(value, 0, width, axis=dim)
        before = lax.ppermute(last, axis, up)
        after = lax.ppermute(first, axis, down)
        value = jnp.concatenate([before, value, after], axis=dim)
    return value


def box_sum(padded):
    total = padded[:, :-2] + padded[:, 1:-1] + padded[:, 2:]
    total = total[:, :, :-2] + total[:, :, 1:-1] + total[:, :, 2:]
    return total[:, :, :, :-2] + total[:, :, :, 1:-1] + total[:, :, :, 2:]


def colors_of(shape):
    first = lax.broadcasted_iota(jnp.int32, shape, 1) % 2
    second = lax.broadcasted_iota(jnp.int32, shape, 2) % 2
    third = lax.broadcasted_iota(jnp.int32, shape, 3) % 2
    return 4 * first + 2 * second + third


def local_gram(left, right):
    return jnp.einsum("kxzy,lxzy->kl", left, right, precision=lax.Precision.HIGHEST)


def combine(field, mixing):
    return jnp.einsum("kxzy,kl->lxzy", field, mixing, precision=lax.Precision.HIGHEST)


def small_dot(left, right):
    return jnp.dot(left, right, precision=lax.Precision.HIGHEST)


def spd_solve(matrix, target):
    order = matrix.shape[0]
    sym = 0.5 * (matrix + matrix.T)
    lower = jnp.zeros_like(sym)
    for col in range(order):
        column = sym[col:, col] - jnp.sum(lower[col:, :col] * lower[col, :col][None, :], axis=1)
        pivot = jnp.sqrt(column[0])
        lower = lower.at[col:, col].set(column / pivot)
    middle = jnp.zeros_like(target)
    for row in range(order):
        value = target[row] - jnp.sum(lower[row, :row][:, None] * middle[:row], axis=0)
        middle = middle.at[row].set(value / lower[row, row])
    answer = jnp.zeros_like(target)
    for row in range(order - 1, -1, -1):
        value = middle[row] - jnp.sum(lower[row + 1 :, row][:, None] * answer[row + 1 :], axis=0)
        answer = answer.at[row].set(value / lower[row, row])
    return answer


def sweep_box(field):
    padded = with_halo(field, (("gx", 1), ("gy", 3), ("gz", 2)), 1)
    return box_sum(padded)


def body(solution, residual, direction_prev, image_prev, gram_prev):
    colors = colors_of(residual.shape)
    smoothed = jnp.where(colors == 0, residual / 26.0, jnp.float32(0.0))
    for shade in list(range(1, 8)) + list(range(6, -1, -1)):
        boxed = sweep_box(smoothed)
        smoothed = jnp.where(colors == shade, (residual + boxed - smoothed) / 26.0, smoothed)
    padded = with_halo(smoothed, (("gx", 1), ("gy", 3), ("gz", 2)), 1)
    image = 27.0 * smoothed - box_sum(padded)
    sums = (
        local_gram(smoothed, residual),
        local_gram(smoothed, image),
        local_gram(smoothed, image_prev),
        local_gram(direction_prev, image),
        local_gram(direction_prev, image_prev),
    )
    gram_zr, gram_zw, gram_zq, gram_pw, gram_pq = lax.psum(
        (sums[0], sums[1], sums[2], sums[3], sums[4]), ("gx", "gy", "gz")
    )
    beta_mix = spd_solve(gram_prev, gram_zr)
    direction = smoothed + combine(direction_prev, beta_mix)
    image_new = image + combine(image_prev, beta_mix)
    curvature = gram_zw + small_dot(gram_zq, beta_mix) + small_dot(beta_mix.T, gram_pw)
    curvature = curvature + small_dot(small_dot(beta_mix.T, gram_pq), beta_mix)
    alpha_step = spd_solve(curvature, gram_zr)
    solution_new = solution + combine(direction, alpha_step)
    residual_new = residual - combine(image_new, alpha_step)
    return (solution_new, residual_new, direction)


def solution(mesh):
    in_specs = (
        P(None, "gx", "gz", "gy"),
        P(None, "gx", "gz", "gy"),
        P(None, "gx", "gz", "gy"),
        P(None, "gx", "gz", "gy"),
        P(),
    )
    out_specs = (P(None, "gx", "gz", "gy"), P(None, "gx", "gz", "gy"), P(None, "gx", "gz", "gy"))
    return jax.shard_map(body, mesh=mesh, in_specs=in_specs, out_specs=out_specs, check_vma=False)
```

profile of v0, /device:TPU:0, one launch (start us, length us, event | category | flops | bytes accessed | tf_op | source)
XLA Modules:
  0.0 495.2 jit_solution(12396959425501181571)
XLA Ops:
  3.0 3.0 collective-permute-start
  21.4 4.9 collective-permute-start.2
  27.4 1.7 collective-permute-done.2
  30.6 6.1 %collective-permute-start.4 = (f32[16,4,1,130]{3,0,2,1:T(8,128)S(1)}, f32[16,4,1,130]{3,0,2,1:T(8,128)S(1)}, u32[]{:S(2)}, u32[]{:S(2)}) collective-permute-start(f32[16,4,1,130]{3,0,2,1:T(8,128)S(1)} %get-tuple-element.1202), channel_id=1, source_target_pairs={{0,1},{1,2},{2,3},{4,5},{5,6},{6,7},{8,9},{9,10},{10,11},{12,13},{... | collective-permute-start | bytes 99848 | tf_op jit(solution)/shard_map/ppermute | solution.py:14
  41.1 3.0 collective-permute-start.6
  46.4 4.6 collective-permute-start.8
  50.9 2.1 collective-permute-done.9
  55.6 4.8 collective-permute-start.10
  60.7 1.6 collective-permute-done.10
  64.0 3.0 collective-permute-start.12
  69.3 4.6 collective-permute-start.14
  75.4 1.7 collective-permute-done.14
  78.5 4.9 collective-permute-start.16
  87.3 3.0 collective-permute-start.18
  92.6 4.6 collective-permute-start.20
  101.1 5.0 %collective-permute-start.22 = (f32[16,4,1,130]{3,0,2,1:T(8,128)S(1)}, f32[16,4,1,130]{3,0,2,1:T(8,128)S(1)}, u32[]{:S(2)}, u32[]{:S(2)}) collective-permute-start(f32[16,4,1,130]{3,0,2,1:T(8,128)S(1)} %get-tuple-element.1196), channel_id=1, source_target_pairs={{0,1},{1,2},{2,3},{4,5},{5,6},{6,7},{8,9},{9,10},{10,11},{12,13},{... | collective-permute-start | bytes 99848 | tf_op jit(solution)/shard_map/ppermute | solution.py:14
  106.4 1.6 collective-permute-done.22
  109.8 3.2 collective-permute-start.24
  115.2 4.6 collective-permute-start.26
  123.7 5.0 %collective-permute-start.28 = (f32[16,4,1,130]{3,0,2,1:T(8,128)S(1)}, f32[16,4,1,130]{3,0,2,1:T(8,128)S(1)}, u32[]{:S(2)}, u32[]{:S(2)}) collective-permute-start(f32[16,4,1,130]{3,0,2,1:T(8,128)S(1)} %get-tuple-element.1194), channel_id=1, source_target_pairs={{0,1},{1,2},{2,3},{4,5},{5,6},{6,7},{8,9},{9,10},{10,11},{12,13},{... | collective-permute-start | bytes 99848 | tf_op jit(solution)/shard_map/ppermute | solution.py:14
  129.0 1.6 collective-permute-done.28
  132.2 4.9 collective-permute-start.30
  139.4 4.6 collective-permute-start.32
  147.9 4.6 collective-permute-start.34
  152.8 1.6 collective-permute-done.34
  156.0 5.3 %collective-permute-start.36 = (f32[16,1,4,128]{3,0,2,1:T(8,128)S(1)}, f32[16,1,4,128]{3,0,2,1:T(8,128)S(1)}, u32[]{:S(2)}, u32[]{:S(2)}) collective-permute-start(f32[16,1,4,128]{3,0,2,1:T(8,128)S(1)} %get-tuple-element.1250), channel_id=1, source_target_pairs={{0,8},{8,16},{16,24},{1,9},{9,17},{17,25},{2,10},{10,18},{18,26},{... | collective-permute-start | bytes 98312 | tf_op jit(solution)/shard_map/ppermute | solution.py:14
  163.6 4.6 collective-permute-start.38
  172.1 4.6 collective-permute-start.40
  177.0 1.6 collective-permute-done.40
  180.3 5.3 %collective-permute-start.42 = (f32[16,1,4,128]{3,0,2,1:T(8,128)S(1)}, f32[16,1,4,128]{3,0,2,1:T(8,128)S(1)}, u32[]{:S(2)}, u32[]{:S(2)}) collective-permute-start(f32[16,1,4,128]{3,0,2,1:T(8,128)S(1)} %get-tuple-element.1248), channel_id=1, source_target_pairs={{0,8},{8,16},{16,24},{1,9},{9,17},{17,25},{2,10},{10,18},{18,26},{... | collective-permute-start | bytes 98312 | tf_op jit(solution)/shard_map/ppermute | solution.py:14
  187.8 4.6 collective-permute-start.44
  196.3 4.8 collective-permute-start.46
  201.2 1.6 collective-permute-done.46
  204.5 5.3 %collective-permute-start.48 = (f32[16,1,4,128]{3,0,2,1:T(8,128)S(1)}, f32[16,1,4,128]{3,0,2,1:T(8,128)S(1)}, u32[]{:S(2)}, u32[]{:S(2)}) collective-permute-start(f32[16,1,4,128]{3,0,2,1:T(8,128)S(1)} %get-tuple-element.1246), channel_id=1, source_target_pairs={{0,8},{8,16},{16,24},{1,9},{9,17},{17,25},{2,10},{10,18},{18,26},{... | collective-permute-start | bytes 98312 | tf_op jit(solution)/shard_map/ppermute | solution.py:14
  212.1 4.6 collective-permute-start.50
  220.5 4.6 collective-permute-start.52
  225.5 1.6 collective-permute-done.52
  228.7 5.3 %collective-permute-start.54 = (f32[16,1,4,128]{3,0,2,1:T(8,128)S(1)}, f32[16,1,4,128]{3,0,2,1:T(8,128)S(1)}, u32[]{:S(2)}, u32[]{:S(2)}) collective-permute-start(f32[16,1,4,128]{3,0,2,1:T(8,128)S(1)} %get-tuple-element.1244), channel_id=1, source_target_pairs={{0,8},{8,16},{16,24},{1,9},{9,17},{17,25},{2,10},{10,18},{18,26},{... | collective-permute-start | bytes 98312 | tf_op jit(solution)/shard_map/ppermute | solution.py:14
  236.3 4.6 collective-permute-start.56
  244.8 4.6 collective-permute-start.58
  249.7 1.6 collective-permute-done.58
  253.0 5.3 %collective-permute-start.60 = (f32[16,1,4,128]{3,0,2,1:T(8,128)S(1)}, f32[16,1,4,128]{3,0,2,1:T(8,128)S(1)}, u32[]{:S(2)}, u32[]{:S(2)}) collective-permute-start(f32[16,1,4,128]{3,0,2,1:T(8,128)S(1)} %get-tuple-element.1242), channel_id=1, source_target_pairs={{0,8},{8,16},{16,24},{1,9},{9,17},{17,25},{2,10},{10,18},{18,26},{... | collective-permute-start | bytes 98312 | tf_op jit(solution)/shard_map/ppermute | solution.py:14
  260.5 4.6 collective-permute-start.62
  269.0 4.6 collective-permute-start.64
  273.9 1.6 collective-permute-done.64
  277.2 5.3 %collective-permute-start.66 = (f32[16,1,4,128]{3,0,2,1:T(8,128)S(1)}, f32[16,1,4,128]{3,0,2,1:T(8,128)S(1)}, u32[]{:S(2)}, u32[]{:S(2)}) collective-permute-start(f32[16,1,4,128]{3,0,2,1:T(8,128)S(1)} %get-tuple-element.1240), channel_id=1, source_target_pairs={{0,8},{8,16},{16,24},{1,9},{9,17},{17,25},{2,10},{10,18},{18,26},{... | collective-permute-start | bytes 98312 | tf_op jit(solution)/shard_map/ppermute | solution.py:14
  284.8 4.6 collective-permute-start.68
  293.2 4.6 collective-permute-start.70
  298.2 1.6 collective-permute-done.70
  301.4 5.3 %collective-permute-start.72 = (f32[16,1,4,128]{3,0,2,1:T(8,128)S(1)}, f32[16,1,4,128]{3,0,2,1:T(8,128)S(1)}, u32[]{:S(2)}, u32[]{:S(2)}) collective-permute-start(f32[16,1,4,128]{3,0,2,1:T(8,128)S(1)} %get-tuple-element.1238), channel_id=1, source_target_pairs={{0,8},{8,16},{16,24},{1,9},{9,17},{17,25},{2,10},{10,18},{18,26},{... | collective-permute-start | bytes 98312 | tf_op jit(solution)/shard_map/ppermute | solution.py:14
  309.0 4.6 collective-permute-start.74
  317.5 4.6 collective-permute-start.76
  322.4 1.6 collective-permute-done.76
  325.6 5.3 %collective-permute-start.78 = (f32[16,1,4,128]{3,0,2,1:T(8,128)S(1)}, f32[16,1,4,128]{3,0,2,1:T(8,128)S(1)}, u32[]{:S(2)}, u32[]{:S(2)}) collective-permute-start(f32[16,1,4,128]{3,0,2,1:T(8,128)S(1)} %get-tuple-element.1236), channel_id=1, source_target_pairs={{0,8},{8,16},{16,24},{1,9},{9,17},{17,25},{2,10},{10,18},{18,26},{... | collective-permute-start | bytes 98312 | tf_op jit(solution)/shard_map/ppermute | solution.py:14
  333.2 4.6 collective-permute-start.80
  341.7 4.6 collective-permute-start.82
  346.6 1.6 collective-permute-done.82
  349.9 5.3 %collective-permute-start.84 = (f32[16,1,4,128]{3,0,2,1:T(8,128)S(1)}, f32[16,1,4,128]{3,0,2,1:T(8,128)S(1)}, u32[]{:S(2)}, u32[]{:S(2)}) collective-permute-start(f32[16,1,4,128]{3,0,2,1:T(8,128)S(1)} %get-tuple-element.1234), channel_id=1, source_target_pairs={{0,8},{8,16},{16,24},{1,9},{9,17},{17,25},{2,10},{10,18},{18,26},{... | collective-permute-start | bytes 98312 | tf_op jit(solution)/shard_map/ppermute | solution.py:14
  358.5 4.6 collective-permute-start.86
  367.0 4.6 collective-permute-start.88
  371.9 1.6 collective-permute-done.88
  374.2 47.6 %all-reduce.6 = (f32[16,16]{1,0:T(8,128)S(1)}, f32[16,16]{1,0:T(8,128)S(1)}, f32[16,16]{1,0:T(8,128)S(1)}, f32[16,16]{0,1:T(8,128)S(1)}, f32[16,16]{1,0:T(8,128)S(1)}) all-reduce(f32[16,16]{1,0:T(8,128)S(1)} %convolution_bitcast_fusion.4, ...), channel_id=1, replica_groups=mesh['gx'=4,'gy'=2,'gz'=4] {'gx','gy','gz'}, use_global_device_ids=true, to_apply=%region_0.1 | all-reduce | flops 1280 | bytes 10240 | tf_op jit(solution)/shard_map/psum | solution.py:84
  421.8 1.9 subtract_divide_fusion.29
  467.4 1.9 subtract_divide_fusion.27
  (709 shorter events, 197.7 us)
Async XLA Ops:
  1.7 18.3 %collective-permute-start.1 = (f32[16,1,4,128]{3,0,2,1:T(8,128)S(1)}, f32[16,1,4,128]{3,0,2,1:T(8,128)S(1)}, u32[]{:S(2)}, u32[]{:S(2)}) collective-permute-start(f32[16,1,4,128]{3,0,2,1:T(8,128)S(1)} %get-tuple-element.1263), channel_id=1, source_target_pairs={{8,0},{16,8},{24,16},{9,1},{17,9},{25,17},{10,2},{18,10},{26,18},{... | collective-permute-start | bytes 98312 | tf_op jit(solution)/shard_map/ppermute | solution.py:15
  3.0 17.0 %collective-permute-start = (f32[16,1,4,128]{3,0,2,1:T(8,128)S(1)}, f32[16,1,4,128]{3,0,2,1:T(8,128)S(1)}, u32[]{:S(2)}, u32[]{:S(2)}) collective-permute-start(f32[16,1,4,128]{3,0,2,1:T(8,128)S(1)} %get-tuple-element.1262), channel_id=1, source_target_pairs={{0,8},{8,16},{16,24},{1,9},{9,17},{17,25},{2,10},{10,18},{18,26},{... | collective-permute-start | bytes 98312 | tf_op jit(solution)/shard_map/ppermute | solution.py:14
  20.1 7.4 %collective-permute-start.3 = (f32[16,4,4,1]{3,0,2,1:T(8,128)S(1)}, f32[16,4,4,1]{3,0,2,1:T(8,128)S(1)}, u32[]{:S(2)}, u32[]{:S(2)}) collective-permute-start(f32[16,4,4,1]{3,0,2,1:T(8,128)S(1)} %get-tuple-element.1233), channel_id=1, source_target_pairs={{4,0},{5,1},{6,2},{7,3},{12,8},{13,9},{14,10},{15,11},{20,16},{21,... | collective-permute-start | bytes 3080 | tf_op jit(solution)/shard_map/ppermute | solution.py:15
  21.4 7.8 %collective-permute-start.2 = (f32[16,4,4,1]{3,0,2,1:T(8,128)S(1)}, f32[16,4,4,1]{3,0,2,1:T(8,128)S(1)}, u32[]{:S(2)}, u32[]{:S(2)}) collective-permute-start(f32[16,4,4,1]{3,0,2,1:T(8,128)S(1)} %get-tuple-element.1232), channel_id=1, source_target_pairs={{0,4},{1,5},{2,6},{3,7},{8,12},{9,13},{10,14},{11,15},{16,20},{17,... | collective-permute-start | bytes 3080 | tf_op jit(solution)/shard_map/ppermute | solution.py:14
  29.3 7.8 %collective-permute-start.5 = (f32[16,4,1,130]{3,0,2,1:T(8,128)S(1)}, f32[16,4,1,130]{3,0,2,1:T(8,128)S(1)}, u32[]{:S(2)}, u32[]{:S(2)}) collective-permute-start(f32[16,4,1,130]{3,0,2,1:T(8,128)S(1)} %get-tuple-element.1203), channel_id=1, source_target_pairs={{1,0},{2,1},{3,2},{5,4},{6,5},{7,6},{9,8},{10,9},{11,10},{13,12},{... | collective-permute-start | bytes 99848 | tf_op jit(solution)/shard_map/ppermute | solution.py:15
  30.6 8.0 %collective-permute-start.4 = (f32[16,4,1,130]{3,0,2,1:T(8,128)S(1)}, f32[16,4,1,130]{3,0,2,1:T(8,128)S(1)}, u32[]{:S(2)}, u32[]{:S(2)}) collective-permute-start(f32[16,4,1,130]{3,0,2,1:T(8,128)S(1)} %get-tuple-element.1202), channel_id=1, source_target_pairs={{0,1},{1,2},{2,3},{4,5},{5,6},{6,7},{8,9},{9,10},{10,11},{12,13},{... | collective-permute-start | bytes 99848 | tf_op jit(solution)/shard_map/ppermute | solution.py:14
  45.1 7.9 %collective-permute-start.9 = (f32[16,4,4,1]{3,0,2,1:T(8,128)S(1)}, f32[16,4,4,1]{3,0,2,1:T(8,128)S(1)}, u32[]{:S(2)}, u32[]{:S(2)}) collective-permute-start(f32[16,4,4,1]{3,0,2,1:T(8,128)S(1)} %get-tuple-element.1231), channel_id=1, source_target_pairs={{4,0},{5,1},{6,2},{7,3},{12,8},{13,9},{14,10},{15,11},{20,16},{21,... | collective-permute-start | bytes 3080 | tf_op jit(solution)/shard_map/ppermute | solution.py:15
  46.4 7.8 %collective-permute-start.8 = (f32[16,4,4,1]{3,0,2,1:T(8,128)S(1)}, f32[16,4,4,1]{3,0,2,1:T(8,128)S(1)}, u32[]{:S(2)}, u32[]{:S(2)}) collective-permute-start(f32[16,4,4,1]{3,0,2,1:T(8,128)S(1)} %get-tuple-element.1230), channel_id=1, source_target_pairs={{0,4},{1,5},{2,6},{3,7},{8,12},{9,13},{10,14},{11,15},{16,20},{17,... | collective-permute-start | bytes 3080 | tf_op jit(solution)/shard_map/ppermute | solution.py:14
  54.3 6.4 %collective-permute-start.11 = (f32[16,4,1,130]{3,0,2,1:T(8,128)S(1)}, f32[16,4,1,130]{3,0,2,1:T(8,128)S(1)}, u32[]{:S(2)}, u32[]{:S(2)}) collective-permute-start(f32[16,4,1,130]{3,0,2,1:T(8,128)S(1)} %get-tuple-element.1201), channel_id=1, source_target_pairs={{1,0},{2,1},{3,2},{5,4},{6,5},{7,6},{9,8},{10,9},{11,10},{13,12},{... | collective-permute-start | bytes 99848 | tf_op jit(solution)/shard_map/ppermute | solution.py:15
  55.6 6.7 %collective-permute-start.10 = (f32[16,4,1,130]{3,0,2,1:T(8,128)S(1)}, f32[16,4,1,130]{3,0,2,1:T(8,128)S(1)}, u32[]{:S(2)}, u32[]{:S(2)}) collective-permute-start(f32[16,4,1,130]{3,0,2,1:T(8,128)S(1)} %get-tuple-element.1200), channel_id=1, source_target_pairs={{0,1},{1,2},{2,3},{4,5},{5,6},{6,7},{8,9},{9,10},{10,11},{12,13},{... | collective-permute-start | bytes 99848 | tf_op jit(solution)/shard_map/ppermute | solution.py:14
  68.0 7.4 %collective-permute-start.15 = (f32[16,4,4,1]{3,0,2,1:T(8,128)S(1)}, f32[16,4,4,1]{3,0,2,1:T(8,128)S(1)}, u32[]{:S(2)}, u32[]{:S(2)}) collective-permute-start(f32[16,4,4,1]{3,0,2,1:T(8,128)S(1)} %get-tuple-element.1229), channel_id=1, source_target_pairs={{4,0},{5,1},{6,2},{7,3},{12,8},{13,9},{14,10},{15,11},{20,16},{21,... | collective-permute-start | bytes 3080 | tf_op jit(solution)/shard_map/ppermute | solution.py:15
  69.3 7.8 %collective-permute-start.14 = (f32[16,4,4,1]{3,0,2,1:T(8,128)S(1)}, f32[16,4,4,1]{3,0,2,1:T(8,128)S(1)}, u32[]{:S(2)}, u32[]{:S(2)}) collective-permute-start(f32[16,4,4,1]{3,0,2,1:T(8,128)S(1)} %get-tuple-element.1228), channel_id=1, source_target_pairs={{0,4},{1,5},{2,6},{3,7},{8,12},{9,13},{10,14},{11,15},{16,20},{17,... | collective-permute-start | bytes 3080 | tf_op jit(solution)/shard_map/ppermute | solution.py:14
  77.2 7.2 %collective-permute-start.17 = (f32[16,4,1,130]{3,0,2,1:T(8,128)S(1)}, f32[16,4,1,130]{3,0,2,1:T(8,128)S(1)}, u32[]{:S(2)}, u32[]{:S(2)}) collective-permute-start(f32[16,4,1,130]{3,0,2,1:T(8,128)S(1)} %get-tuple-element.1199), channel_id=1, source_target_pairs={{1,0},{2,1},{3,2},{5,4},{6,5},{7,6},{9,8},{10,9},{11,10},{13,12},{... | collective-permute-start | bytes 99848 | tf_op jit(solution)/shard_map/ppermute | solution.py:15
  78.5 7.1 %collective-permute-start.16 = (f32[16,4,1,130]{3,0,2,1:T(8,128)S(1)}, f32[16,4,1,130]{3,0,2,1:T(8,128)S(1)}, u32[]{:S(2)}, u32[]{:S(2)}) collective-permute-start(f32[16,4,1,130]{3,0,2,1:T(8,128)S(1)} %get-tuple-element.1198), channel_id=1, source_target_pairs={{0,1},{1,2},{2,3},{4,5},{5,6},{6,7},{8,9},{9,10},{10,11},{12,13},{... | collective-permute-start | bytes 99848 | tf_op jit(solution)/shard_map/ppermute | solution.py:14
  91.3 6.9 %collective-permute-start.21 = (f32[16,4,4,1]{3,0,2,1:T(8,128)S(1)}, f32[16,4,4,1]{3,0,2,1:T(8,128)S(1)}, u32[]{:S(2)}, u32[]{:S(2)}) collective-permute-start(f32[16,4,4,1]{3,0,2,1:T(8,128)S(1)} %get-tuple-element.1227), channel_id=1, source_target_pairs={{4,0},{5,1},{6,2},{7,3},{12,8},{13,9},{14,10},{15,11},{20,16},{21,... | collective-permute-start | bytes 3080 | tf_op jit(solution)/shard_map/ppermute | solution.py:15
  92.6 7.1 %collective-permute-start.20 = (f32[16,4,4,1]{3,0,2,1:T(8,128)S(1)}, f32[16,4,4,1]{3,0,2,1:T(8,128)S(1)}, u32[]{:S(2)}, u32[]{:S(2)}) collective-permute-start(f32[16,4,4,1]{3,0,2,1:T(8,128)S(1)} %get-tuple-element.1226), channel_id=1, source_target_pairs={{0,4},{1,5},{2,6},{3,7},{8,12},{9,13},{10,14},{11,15},{16,20},{17,... | collective-permute-start | bytes 3080 | tf_op jit(solution)/shard_map/ppermute | solution.py:14
  99.8 6.6 %collective-permute-start.23 = (f32[16,4,1,130]{3,0,2,1:T(8,128)S(1)}, f32[16,4,1,130]{3,0,2,1:T(8,128)S(1)}, u32[]{:S(2)}, u32[]{:S(2)}) collective-permute-start(f32[16,4,1,130]{3,0,2,1:T(8,128)S(1)} %get-tuple-element.1197), channel_id=1, source_target_pairs={{1,0},{2,1},{3,2},{5,4},{6,5},{7,6},{9,8},{10,9},{11,10},{13,12},{... | collective-permute-start | bytes 99848 | tf_op jit(solution)/shard_map/ppermute | solution.py:15
  101.1 7.0 %collective-permute-start.22 = (f32[16,4,1,130]{3,0,2,1:T(8,128)S(1)}, f32[16,4,1,130]{3,0,2,1:T(8,128)S(1)}, u32[]{:S(2)}, u32[]{:S(2)}) collective-permute-start(f32[16,4,1,130]{3,0,2,1:T(8,128)S(1)} %get-tuple-element.1196), channel_id=1, source_target_pairs={{0,1},{1,2},{2,3},{4,5},{5,6},{6,7},{8,9},{9,10},{10,11},{12,13},{... | collective-permute-start | bytes 99848 | tf_op jit(solution)/shard_map/ppermute | solution.py:14
  113.9 6.9 %collective-permute-start.27 = (f32[16,4,4,1]{3,0,2,1:T(8,128)S(1)}, f32[16,4,4,1]{3,0,2,1:T(8,128)S(1)}, u32[]{:S(2)}, u32[]{:S(2)}) collective-permute-start(f32[16,4,4,1]{3,0,2,1:T(8,128)S(1)} %get-tuple-element.1225), channel_id=1, source_target_pairs={{4,0},{5,1},{6,2},{7,3},{12,8},{13,9},{14,10},{15,11},{20,16},{21,... | collective-permute-start | bytes 3080 | tf_op jit(solution)/shard_map/ppermute | solution.py:15
  115.2 7.1 %collective-permute-start.26 = (f32[16,4,4,1]{3,0,2,1:T(8,128)S(1)}, f32[16,4,4,1]{3,0,2,1:T(8,128)S(1)}, u32[]{:S(2)}, u32[]{:S(2)}) collective-permute-start(f32[16,4,4,1]{3,0,2,1:T(8,128)S(1)} %get-tuple-element.1224), channel_id=1, source_target_pairs={{0,4},{1,5},{2,6},{3,7},{8,12},{9,13},{10,14},{11,15},{16,20},{17,... | collective-permute-start | bytes 3080 | tf_op jit(solution)/shard_map/ppermute | solution.py:14
  122.4 6.6 %collective-permute-start.29 = (f32[16,4,1,130]{3,0,2,1:T(8,128)S(1)}, f32[16,4,1,130]{3,0,2,1:T(8,128)S(1)}, u32[]{:S(2)}, u32[]{:S(2)}) collective-permute-start(f32[16,4,1,130]{3,0,2,1:T(8,128)S(1)} %get-tuple-element.1195), channel_id=1, source_target_pairs={{1,0},{2,1},{3,2},{5,4},{6,5},{7,6},{9,8},{10,9},{11,10},{13,12},{... | collective-permute-start | bytes 99848 | tf_op jit(solution)/shard_map/ppermute | solution.py:15
  123.7 6.9 %collective-permute-start.28 = (f32[16,4,1,130]{3,0,2,1:T(8,128)S(1)}, f32[16,4,1,130]{3,0,2,1:T(8,128)S(1)}, u32[]{:S(2)}, u32[]{:S(2)}) collective-permute-start(f32[16,4,1,130]{3,0,2,1:T(8,128)S(1)} %get-tuple-element.1194), channel_id=1, source_target_pairs={{0,1},{1,2},{2,3},{4,5},{5,6},{6,7},{8,9},{9,10},{10,11},{12,13},{... | collective-permute-start | bytes 99848 | tf_op jit(solution)/shard_map/ppermute | solution.py:14
  138.1 6.9 %collective-permute-start.33 = (f32[16,4,4,1]{3,0,2,1:T(8,128)S(1)}, f32[16,4,4,1]{3,0,2,1:T(8,128)S(1)}, u32[]{:S(2)}, u32[]{:S(2)}) collective-permute-start(f32[16,4,4,1]{3,0,2,1:T(8,128)S(1)} %get-tuple-element.1223), channel_id=1, source_target_pairs={{4,0},{5,1},{6,2},{7,3},{12,8},{13,9},{14,10},{15,11},{20,16},{21,... | collective-permute-start | bytes 3080 | tf_op jit(solution)/shard_map/ppermute | solution.py:15
  139.4 7.1 %collective-permute-start.32 = (f32[16,4,4,1]{3,0,2,1:T(8,128)S(1)}, f32[16,4,4,1]{3,0,2,1:T(8,128)S(1)}, u32[]{:S(2)}, u32[]{:S(2)}) collective-permute-start(f32[16,4,4,1]{3,0,2,1:T(8,128)S(1)} %get-tuple-element.1222), channel_id=1, source_target_pairs={{0,4},{1,5},{2,6},{3,7},{8,12},{9,13},{10,14},{11,15},{16,20},{17,... | collective-permute-start | bytes 3080 | tf_op jit(solution)/shard_map/ppermute | solution.py:14
  146.6 6.2 %collective-permute-start.35 = (f32[16,4,1,130]{3,0,2,1:T(8,128)S(1)}, f32[16,4,1,130]{3,0,2,1:T(8,128)S(1)}, u32[]{:S(2)}, u32[]{:S(2)}) collective-permute-start(f32[16,4,1,130]{3,0,2,1:T(8,128)S(1)} %get-tuple-element.1193), channel_id=1, source_target_pairs={{1,0},{2,1},{3,2},{5,4},{6,5},{7,6},{9,8},{10,9},{11,10},{13,12},{... | collective-permute-start | bytes 99848 | tf_op jit(solution)/shard_map/ppermute | solution.py:15
  147.9 6.5 %collective-permute-start.34 = (f32[16,4,1,130]{3,0,2,1:T(8,128)S(1)}, f32[16,4,1,130]{3,0,2,1:T(8,128)S(1)}, u32[]{:S(2)}, u32[]{:S(2)}) collective-permute-start(f32[16,4,1,130]{3,0,2,1:T(8,128)S(1)} %get-tuple-element.1192), channel_id=1, source_target_pairs={{0,1},{1,2},{2,3},{4,5},{5,6},{6,7},{8,9},{9,10},{10,11},{12,13},{... | collective-permute-start | bytes 99848 | tf_op jit(solution)/shard_map/ppermute | solution.py:14
  154.7 6.6 %collective-permute-start.37 = (f32[16,1,4,128]{3,0,2,1:T(8,128)S(1)}, f32[16,1,4,128]{3,0,2,1:T(8,128)S(1)}, u32[]{:S(2)}, u32[]{:S(2)}) collective-permute-start(f32[16,1,4,128]{3,0,2,1:T(8,128)S(1)} %get-tuple-element.1251), channel_id=1, source_target_pairs={{8,0},{16,8},{24,16},{9,1},{17,9},{25,17},{10,2},{18,10},{26,18},{... | collective-permute-start | bytes 98312 | tf_op jit(solution)/shard_map/ppermute | solution.py:15
  162.3 6.9 %collective-permute-start.39 = (f32[16,4,4,1]{3,0,2,1:T(8,128)S(1)}, f32[16,4,4,1]{3,0,2,1:T(8,128)S(1)}, u32[]{:S(2)}, u32[]{:S(2)}) collective-permute-start(f32[16,4,4,1]{3,0,2,1:T(8,128)S(1)} %get-tuple-element.1221), channel_id=1, source_target_pairs={{4,0},{5,1},{6,2},{7,3},{12,8},{13,9},{14,10},{15,11},{20,16},{21,... | collective-permute-start | bytes 3080 | tf_op jit(solution)/shard_map/ppermute | solution.py:15
  163.6 7.1 %collective-permute-start.38 = (f32[16,4,4,1]{3,0,2,1:T(8,128)S(1)}, f32[16,4,4,1]{3,0,2,1:T(8,128)S(1)}, u32[]{:S(2)}, u32[]{:S(2)}) collective-permute-start(f32[16,4,4,1]{3,0,2,1:T(8,128)S(1)} %get-tuple-element.1220), channel_id=1, source_target_pairs={{0,4},{1,5},{2,6},{3,7},{8,12},{9,13},{10,14},{11,15},{16,20},{17,... | collective-permute-start | bytes 3080 | tf_op jit(solution)/shard_map/ppermute | solution.py:14
  170.8 6.2 %collective-permute-start.41 = (f32[16,4,1,130]{3,0,2,1:T(8,128)S(1)}, f32[16,4,1,130]{3,0,2,1:T(8,128)S(1)}, u32[]{:S(2)}, u32[]{:S(2)}) collective-permute-start(f32[16,4,1,130]{3,0,2,1:T(8,128)S(1)} %get-tuple-element.1191), channel_id=1, source_target_pairs={{1,0},{2,1},{3,2},{5,4},{6,5},{7,6},{9,8},{10,9},{11,10},{13,12},{... | collective-permute-start | bytes 99848 | tf_op jit(solution)/shard_map/ppermute | solution.py:15
  172.1 6.5 %collective-permute-start.40 = (f32[16,4,1,130]{3,0,2,1:T(8,128)S(1)}, f32[16,4,1,130]{3,0,2,1:T(8,128)S(1)}, u32[]{:S(2)}, u32[]{:S(2)}) collective-permute-start(f32[16,4,1,130]{3,0,2,1:T(8,128)S(1)} %get-tuple-element.1190), channel_id=1, source_target_pairs={{0,1},{1,2},{2,3},{4,5},{5,6},{6,7},{8,9},{9,10},{10,11},{12,13},{... | collective-permute-start | bytes 99848 | tf_op jit(solution)/shard_map/ppermute | solution.py:14
  179.0 6.6 %collective-permute-start.43 = (f32[16,1,4,128]{3,0,2,1:T(8,128)S(1)}, f32[16,1,4,128]{3,0,2,1:T(8,128)S(1)}, u32[]{:S(2)}, u32[]{:S(2)}) collective-permute-start(f32[16,1,4,128]{3,0,2,1:T(8,128)S(1)} %get-tuple-element.1249), channel_id=1, source_target_pairs={{8,0},{16,8},{24,16},{9,1},{17,9},{25,17},{10,2},{18,10},{26,18},{... | collective-permute-start | bytes 98312 | tf_op jit(solution)/shard_map/ppermute | solution.py:15
  186.5 6.9 %collective-permute-start.45 = (f32[16,4,4,1]{3,0,2,1:T(8,128)S(1)}, f32[16,4,4,1]{3,0,2,1:T(8,128)S(1)}, u32[]{:S(2)}, u32[]{:S(2)}) collective-permute-start(f32[16,4,4,1]{3,0,2,1:T(8,128)S(1)} %get-tuple-element.1219), channel_id=1, source_target_pairs={{4,0},{5,1},{6,2},{7,3},{12,8},{13,9},{14,10},{15,11},{20,16},{21,... | collective-permute-start | bytes 3080 | tf_op jit(solution)/shard_map/ppermute | solution.py:15
  187.8 7.1 %collective-permute-start.44 = (f32[16,4,4,1]{3,0,2,1:T(8,128)S(1)}, f32[16,4,4,1]{3,0,2,1:T(8,128)S(1)}, u32[]{:S(2)}, u32[]{:S(2)}) collective-permute-start(f32[16,4,4,1]{3,0,2,1:T(8,128)S(1)} %get-tuple-element.1218), channel_id=1, source_target_pairs={{0,4},{1,5},{2,6},{3,7},{8,12},{9,13},{10,14},{11,15},{16,20},{17,... | collective-permute-start | bytes 3080 | tf_op jit(solution)/shard_map/ppermute | solution.py:14
  196.3 6.5 %collective-permute-start.46 = (f32[16,4,1,130]{3,0,2,1:T(8,128)S(1)}, f32[16,4,1,130]{3,0,2,1:T(8,128)S(1)}, u32[]{:S(2)}, u32[]{:S(2)}) collective-permute-start(f32[16,4,1,130]{3,0,2,1:T(8,128)S(1)} %get-tuple-element.1188), channel_id=1, source_target_pairs={{0,1},{1,2},{2,3},{4,5},{5,6},{6,7},{8,9},{9,10},{10,11},{12,13},{... | collective-permute-start | bytes 99848 | tf_op jit(solution)/shard_map/ppermute | solution.py:14
  203.2 6.6 %collective-permute-start.49 = (f32[16,1,4,128]{3,0,2,1:T(8,128)S(1)}, f32[16,1,4,128]{3,0,2,1:T(8,128)S(1)}, u32[]{:S(2)}, u32[]{:S(2)}) collective-permute-start(f32[16,1,4,128]{3,0,2,1:T(8,128)S(1)} %get-tuple-element.1247), channel_id=1, source_target_pairs={{8,0},{16,8},{24,16},{9,1},{17,9},{25,17},{10,2},{18,10},{26,18},{... | collective-permute-start | bytes 98312 | tf_op jit(solution)/shard_map/ppermute | solution.py:15
  210.8 6.9 %collective-permute-start.51 = (f32[16,4,4,1]{3,0,2,1:T(8,128)S(1)}, f32[16,4,4,1]{3,0,2,1:T(8,128)S(1)}, u32[]{:S(2)}, u32[]{:S(2)}) collective-permute-start(f32[16,4,4,1]{3,0,2,1:T(8,128)S(1)} %get-tuple-element.1217), channel_id=1, source_target_pairs={{4,0},{5,1},{6,2},{7,3},{12,8},{13,9},{14,10},{15,11},{20,16},{21,... | collective-permute-start | bytes 3080 | tf_op jit(solution)/shard_map/ppermute | solution.py:15
  212.1 7.1 %collective-permute-start.50 = (f32[16,4,4,1]{3,0,2,1:T(8,128)S(1)}, f32[16,4,4,1]{3,0,2,1:T(8,128)S(1)}, u32[]{:S(2)}, u32[]{:S(2)}) collective-permute-start(f32[16,4,4,1]{3,0,2,1:T(8,128)S(1)} %get-tuple-element.1216), channel_id=1, source_target_pairs={{0,4},{1,5},{2,6},{3,7},{8,12},{9,13},{10,14},{11,15},{16,20},{17,... | collective-permute-start | bytes 3080 | tf_op jit(solution)/shard_map/ppermute | solution.py:14
  220.5 6.5 %collective-permute-start.52 = (f32[16,4,1,130]{3,0,2,1:T(8,128)S(1)}, f32[16,4,1,130]{3,0,2,1:T(8,128)S(1)}, u32[]{:S(2)}, u32[]{:S(2)}) collective-permute-start(f32[16,4,1,130]{3,0,2,1:T(8,128)S(1)} %get-tuple-element.1186), channel_id=1, source_target_pairs={{0,1},{1,2},{2,3},{4,5},{5,6},{6,7},{8,9},{9,10},{10,11},{12,13},{... | collective-permute-start | bytes 99848 | tf_op jit(solution)/shard_map/ppermute | solution.py:14
  227.4 7.3 %collective-permute-start.55 = (f32[16,1,4,128]{3,0,2,1:T(8,128)S(1)}, f32[16,1,4,128]{3,0,2,1:T(8,128)S(1)}, u32[]{:S(2)}, u32[]{:S(2)}) collective-permute-start(f32[16,1,4,128]{3,0,2,1:T(8,128)S(1)} %get-tuple-element.1245), channel_id=1, source_target_pairs={{8,0},{16,8},{24,16},{9,1},{17,9},{25,17},{10,2},{18,10},{26,18},{... | collective-permute-start | bytes 98312 | tf_op jit(solution)/shard_map/ppermute | solution.py:15
  235.0 6.9 %collective-permute-start.57 = (f32[16,4,4,1]{3,0,2,1:T(8,128)S(1)}, f32[16,4,4,1]{3,0,2,1:T(8,128)S(1)}, u32[]{:S(2)}, u32[]{:S(2)}) collective-permute-start(f32[16,4,4,1]{3,0,2,1:T(8,128)S(1)} %get-tuple-element.1215), channel_id=1, source_target_pairs={{4,0},{5,1},{6,2},{7,3},{12,8},{13,9},{14,10},{15,11},{20,16},{21,... | collective-permute-start | bytes 3080 | tf_op jit(solution)/shard_map/ppermute | solution.py:15
  236.3 7.1 %collective-permute-start.56 = (f32[16,4,4,1]{3,0,2,1:T(8,128)S(1)}, f32[16,4,4,1]{3,0,2,1:T(8,128)S(1)}, u32[]{:S(2)}, u32[]{:S(2)}) collective-permute-start(f32[16,4,4,1]{3,0,2,1:T(8,128)S(1)} %get-tuple-element.1214), channel_id=1, source_target_pairs={{0,4},{1,5},{2,6},{3,7},{8,12},{9,13},{10,14},{11,15},{16,20},{17,... | collective-permute-start | bytes 3080 | tf_op jit(solution)/shard_map/ppermute | solution.py:14
  244.8 6.5 %collective-permute-start.58 = (f32[16,4,1,130]{3,0,2,1:T(8,128)S(1)}, f32[16,4,1,130]{3,0,2,1:T(8,128)S(1)}, u32[]{:S(2)}, u32[]{:S(2)}) collective-permute-start(f32[16,4,1,130]{3,0,2,1:T(8,128)S(1)} %get-tuple-element.1184), channel_id=1, source_target_pairs={{0,1},{1,2},{2,3},{4,5},{5,6},{6,7},{8,9},{9,10},{10,11},{12,13},{... | collective-permute-start | bytes 99848 | tf_op jit(solution)/shard_map/ppermute | solution.py:14
  251.7 6.8 %collective-permute-start.61 = (f32[16,1,4,128]{3,0,2,1:T(8,128)S(1)}, f32[16,1,4,128]{3,0,2,1:T(8,128)S(1)}, u32[]{:S(2)}, u32[]{:S(2)}) collective-permute-start(f32[16,1,4,128]{3,0,2,1:T(8,128)S(1)} %get-tuple-element.1243), channel_id=1, source_target_pairs={{8,0},{16,8},{24,16},{9,1},{17,9},{25,17},{10,2},{18,10},{26,18},{... | collective-permute-start | bytes 98312 | tf_op jit(solution)/shard_map/ppermute | solution.py:15
  259.2 6.9 %collective-permute-start.63 = (f32[16,4,4,1]{3,0,2,1:T(8,128)S(1)}, f32[16,4,4,1]{3,0,2,1:T(8,128)S(1)}, u32[]{:S(2)}, u32[]{:S(2)}) collective-permute-start(f32[16,4,4,1]{3,0,2,1:T(8,128)S(1)} %get-tuple-element.1213), channel_id=1, source_target_pairs={{4,0},{5,1},{6,2},{7,3},{12,8},{13,9},{14,10},{15,11},{20,16},{21,... | collective-permute-start | bytes 3080 | tf_op jit(solution)/shard_map/ppermute | solution.py:15
  260.5 7.1 %collective-permute-start.62 = (f32[16,4,4,1]{3,0,2,1:T(8,128)S(1)}, f32[16,4,4,1]{3,0,2,1:T(8,128)S(1)}, u32[]{:S(2)}, u32[]{:S(2)}) collective-permute-start(f32[16,4,4,1]{3,0,2,1:T(8,128)S(1)} %get-tuple-element.1212), channel_id=1, source_target_pairs={{0,4},{1,5},{2,6},{3,7},{8,12},{9,13},{10,14},{11,15},{16,20},{17,... | collective-permute-start | bytes 3080 | tf_op jit(solution)/shard_map/ppermute | solution.py:14
  269.0 6.5 %collective-permute-start.64 = (f32[16,4,1,130]{3,0,2,1:T(8,128)S(1)}, f32[16,4,1,130]{3,0,2,1:T(8,128)S(1)}, u32[]{:S(2)}, u32[]{:S(2)}) collective-permute-start(f32[16,4,1,130]{3,0,2,1:T(8,128)S(1)} %get-tuple-element.1182), channel_id=1, source_target_pairs={{0,1},{1,2},{2,3},{4,5},{5,6},{6,7},{8,9},{9,10},{10,11},{12,13},{... | collective-permute-start | bytes 99848 | tf_op jit(solution)/shard_map/ppermute | solution.py:14
  275.9 6.8 %collective-permute-start.67 = (f32[16,1,4,128]{3,0,2,1:T(8,128)S(1)}, f32[16,1,4,128]{3,0,2,1:T(8,128)S(1)}, u32[]{:S(2)}, u32[]{:S(2)}) collective-permute-start(f32[16,1,4,128]{3,0,2,1:T(8,128)S(1)} %get-tuple-element.1241), channel_id=1, source_target_pairs={{8,0},{16,8},{24,16},{9,1},{17,9},{25,17},{10,2},{18,10},{26,18},{... | collective-permute-start | bytes 98312 | tf_op jit(solution)/shard_map/ppermute | solution.py:15
  283.5 6.9 %collective-permute-start.69 = (f32[16,4,4,1]{3,0,2,1:T(8,128)S(1)}, f32[16,4,4,1]{3,0,2,1:T(8,128)S(1)}, u32[]{:S(2)}, u32[]{:S(2)}) collective-permute-start(f32[16,4,4,1]{3,0,2,1:T(8,128)S(1)} %get-tuple-element.1211), channel_id=1, source_target_pairs={{4,0},{5,1},{6,2},{7,3},{12,8},{13,9},{14,10},{15,11},{20,16},{21,... | collective-permute-start | bytes 3080 | tf_op jit(solution)/shard_map/ppermute | solution.py:15
  284.8 7.1 %collective-permute-start.68 = (f32[16,4,4,1]{3,0,2,1:T(8,128)S(1)}, f32[16,4,4,1]{3,0,2,1:T(8,128)S(1)}, u32[]{:S(2)}, u32[]{:S(2)}) collective-permute-start(f32[16,4,4,1]{3,0,2,1:T(8,128)S(1)} %get-tuple-element.1210), channel_id=1, source_target_pairs={{0,4},{1,5},{2,6},{3,7},{8,12},{9,13},{10,14},{11,15},{16,20},{17,... | collective-permute-start | bytes 3080 | tf_op jit(solution)/shard_map/ppermute | solution.py:14
  293.2 6.5 %collective-permute-start.70 = (f32[16,4,1,130]{3,0,2,1:T(8,128)S(1)}, f32[16,4,1,130]{3,0,2,1:T(8,128)S(1)}, u32[]{:S(2)}, u32[]{:S(2)}) collective-permute-start(f32[16,4,1,130]{3,0,2,1:T(8,128)S(1)} %get-tuple-element.1180), channel_id=1, source_target_pairs={{0,1},{1,2},{2,3},{4,5},{5,6},{6,7},{8,9},{9,10},{10,11},{12,13},{... | collective-permute-start | bytes 99848 | tf_op jit(solution)/shard_map/ppermute | solution.py:14
  300.1 6.8 %collective-permute-start.73 = (f32[16,1,4,128]{3,0,2,1:T(8,128)S(1)}, f32[16,1,4,128]{3,0,2,1:T(8,128)S(1)}, u32[]{:S(2)}, u32[]{:S(2)}) collective-permute-start(f32[16,1,4,128]{3,0,2,1:T(8,128)S(1)} %get-tuple-element.1239), channel_id=1, source_target_pairs={{8,0},{16,8},{24,16},{9,1},{17,9},{25,17},{10,2},{18,10},{26,18},{... | collective-permute-start | bytes 98312 | tf_op jit(solution)/shard_map/ppermute | solution.py:15
  307.7 6.9 %collective-permute-start.75 = (f32[16,4,4,1]{3,0,2,1:T(8,128)S(1)}, f32[16,4,4,1]{3,0,2,1:T(8,128)S(1)}, u32[]{:S(2)}, u32[]{:S(2)}) collective-permute-start(f32[16,4,4,1]{3,0,2,1:T(8,128)S(1)} %get-tuple-element.1209), channel_id=1, source_target_pairs={{4,0},{5,1},{6,2},{7,3},{12,8},{13,9},{14,10},{15,11},{20,16},{21,... | collective-permute-start | bytes 3080 | tf_op jit(solution)/shard_map/ppermute | solution.py:15
  309.0 7.1 %collective-permute-start.74 = (f32[16,4,4,1]{3,0,2,1:T(8,128)S(1)}, f32[16,4,4,1]{3,0,2,1:T(8,128)S(1)}, u32[]{:S(2)}, u32[]{:S(2)}) collective-permute-start(f32[16,4,4,1]{3,0,2,1:T(8,128)S(1)} %get-tuple-element.1208), channel_id=1, source_target_pairs={{0,4},{1,5},{2,6},{3,7},{8,12},{9,13},{10,14},{11,15},{16,20},{17,... | collective-permute-start | bytes 3080 | tf_op jit(solution)/shard_map/ppermute | solution.py:14
  317.5 6.5 %collective-permute-start.76 = (f32[16,4,1,130]{3,0,2,1:T(8,128)S(1)}, f32[16,4,1,130]{3,0,2,1:T(8,128)S(1)}, u32[]{:S(2)}, u32[]{:S(2)}) collective-permute-start(f32[16,4,1,130]{3,0,2,1:T(8,128)S(1)} %get-tuple-element.1178), channel_id=1, source_target_pairs={{0,1},{1,2},{2,3},{4,5},{5,6},{6,7},{8,9},{9,10},{10,11},{12,13},{... | collective-permute-start | bytes 99848 | tf_op jit(solution)/shard_map/ppermute | solution.py:14
  324.3 6.8 %collective-permute-start.79 = (f32[16,1,4,128]{3,0,2,1:T(8,128)S(1)}, f32[16,1,4,128]{3,0,2,1:T(8,128)S(1)}, u32[]{:S(2)}, u32[]{:S(2)}) collective-permute-start(f32[16,1,4,128]{3,0,2,1:T(8,128)S(1)} %get-tuple-element.1237), channel_id=1, source_target_pairs={{8,0},{16,8},{24,16},{9,1},{17,9},{25,17},{10,2},{18,10},{26,18},{... | collective-permute-start | bytes 98312 | tf_op jit(solution)/shard_map/ppermute | solution.py:15
  331.9 6.9 %collective-permute-start.81 = (f32[16,4,4,1]{3,0,2,1:T(8,128)S(1)}, f32[16,4,4,1]{3,0,2,1:T(8,128)S(1)}, u32[]{:S(2)}, u32[]{:S(2)}) collective-permute-start(f32[16,4,4,1]{3,0,2,1:T(8,128)S(1)} %get-tuple-element.1207), channel_id=1, source_target_pairs={{4,0},{5,1},{6,2},{7,3},{12,8},{13,9},{14,10},{15,11},{20,16},{21,... | collective-permute-start | bytes 3080 | tf_op jit(solution)/shard_map/ppermute | solution.py:15
  333.2 7.1 %collective-permute-start.80 = (f32[16,4,4,1]{3,0,2,1:T(8,128)S(1)}, f32[16,4,4,1]{3,0,2,1:T(8,128)S(1)}, u32[]{:S(2)}, u32[]{:S(2)}) collective-permute-start(f32[16,4,4,1]{3,0,2,1:T(8,128)S(1)} %get-tuple-element.1206), channel_id=1, source_target_pairs={{0,4},{1,5},{2,6},{3,7},{8,12},{9,13},{10,14},{11,15},{16,20},{17,... | collective-permute-start | bytes 3080 | tf_op jit(solution)/shard_map/ppermute | solution.py:14
  341.7 6.5 %collective-permute-start.82 = (f32[16,4,1,130]{3,0,2,1:T(8,128)S(1)}, f32[16,4,1,130]{3,0,2,1:T(8,128)S(1)}, u32[]{:S(2)}, u32[]{:S(2)}) collective-permute-start(f32[16,4,1,130]{3,0,2,1:T(8,128)S(1)} %get-tuple-element.1176), channel_id=1, source_target_pairs={{0,1},{1,2},{2,3},{4,5},{5,6},{6,7},{8,9},{9,10},{10,11},{12,13},{... | collective-permute-start | bytes 99848 | tf_op jit(solution)/shard_map/ppermute | solution.py:14
  348.6 8.4 %collective-permute-start.85 = (f32[16,1,4,128]{3,0,2,1:T(8,128)S(1)}, f32[16,1,4,128]{3,0,2,1:T(8,128)S(1)}, u32[]{:S(2)}, u32[]{:S(2)}) collective-permute-start(f32[16,1,4,128]{3,0,2,1:T(8,128)S(1)} %get-tuple-element.1235), channel_id=1, source_target_pairs={{8,0},{16,8},{24,16},{9,1},{17,9},{25,17},{10,2},{18,10},{26,18},{... | collective-permute-start | bytes 98312 | tf_op jit(solution)/shard_map/ppermute | solution.py:15
  349.9 7.2 %collective-permute-start.84 = (f32[16,1,4,128]{3,0,2,1:T(8,128)S(1)}, f32[16,1,4,128]{3,0,2,1:T(8,128)S(1)}, u32[]{:S(2)}, u32[]{:S(2)}) collective-permute-start(f32[16,1,4,128]{3,0,2,1:T(8,128)S(1)} %get-tuple-element.1234), channel_id=1, source_target_pairs={{0,8},{8,16},{16,24},{1,9},{9,17},{17,25},{2,10},{10,18},{18,26},{... | collective-permute-start | bytes 98312 | tf_op jit(solution)/shard_map/ppermute | solution.py:14
  357.2 6.9 %collective-permute-start.87 = (f32[16,4,4,1]{3,0,2,1:T(8,128)S(1)}, f32[16,4,4,1]{3,0,2,1:T(8,128)S(1)}, u32[]{:S(2)}, u32[]{:S(2)}) collective-permute-start(f32[16,4,4,1]{3,0,2,1:T(8,128)S(1)} %get-tuple-element.1205), channel_id=1, source_target_pairs={{4,0},{5,1},{6,2},{7,3},{12,8},{13,9},{14,10},{15,11},{20,16},{21,... | collective-permute-start | bytes 3080 | tf_op jit(solution)/shard_map/ppermute | solution.py:15
  358.5 7.1 %collective-permute-start.86 = (f32[16,4,4,1]{3,0,2,1:T(8,128)S(1)}, f32[16,4,4,1]{3,0,2,1:T(8,128)S(1)}, u32[]{:S(2)}, u32[]{:S(2)}) collective-permute-start(f32[16,4,4,1]{3,0,2,1:T(8,128)S(1)} %get-tuple-element.1204), channel_id=1, source_target_pairs={{0,4},{1,5},{2,6},{3,7},{8,12},{9,13},{10,14},{11,15},{16,20},{17,... | collective-permute-start | bytes 3080 | tf_op jit(solution)/shard_map/ppermute | solution.py:14
  367.0 6.5 %collective-permute-start.88 = (f32[16,4,1,130]{3,0,2,1:T(8,128)S(1)}, f32[16,4,1,130]{3,0,2,1:T(8,128)S(1)}, u32[]{:S(2)}, u32[]{:S(2)}) collective-permute-start(f32[16,4,1,130]{3,0,2,1:T(8,128)S(1)} %get-tuple-element.1174), channel_id=1, source_target_pairs={{0,1},{1,2},{2,3},{4,5},{5,6},{6,7},{8,9},{9,10},{10,11},{12,13},{... | collective-permute-start | bytes 99848 | tf_op jit(solution)/shard_map/ppermute | solution.py:14
  (31 other events, 384.0 us)
where the time goes:
time: 498 us; the launch traced here: 495 us
  starting transfers between devices  267 us (54%)
  waiting for transfers between devices  71.8 us (14%)
  other arithmetic  62.7 us (13%)
  blocking collectives  47.6 us (10%)
  local copies, waits for them, and re-layouts  32.4 us (7%)
  between operations  11.3 us (2%)
    ppermute x45, starting transfers between devices, with_halo(): before = lax.ppermute(last, axis, up)  209 us
    ppermute x45, starting transfers between devices, with_halo(): after = lax.ppermute(first, axis, down)  58.1 us
    ppermute x45, waiting for transfers between devices, with_halo(): before = lax.ppermute(last, axis, up)  54.6 us
    psum x1, blocking collectives, body(): lax.psum((sums[0], sums[1], sums[2], sums[3], sums[4]), ('gx', 'gy', 'gz'))  47.6 us
    div x30, other arithmetic, spd_solve(): answer = answer.at[row].set(value / lower[row, row])  20.1 us
    div x28, other arithmetic, spd_solve(): middle = middle.at[row].set(value / lower[row, row])  20.1 us
    ppermute x45, waiting for transfers between devices, with_halo(): after = lax.ppermute(first, axis, down)  17.2 us
  transfers between devices with their start and end apart: 90, of which 71 were waited for; matrix products, arithmetic and copies ran while one was open for 4% of the time, Pallas kernels for 0%

commit v1 on v0

--- a/solution.py
+++ b/solution.py
@@ -1,6 +1,10 @@
+import functools
+
 import jax
 import jax.numpy as jnp
 from jax import lax
+from jax.experimental import pallas as pl
+from jax.experimental.pallas import tpu as pltpu
 from jax.sharding import PartitionSpec as P
 
 
@@ -95,6 +99,288 @@
     return (solution_new, residual_new, direction)
 
 
+MESH = pl.DeviceIdType.MESH
+HIGHEST = lax.Precision.HIGHEST
+
+
+def dot(left, right):
+    return jnp.dot(left, right, precision=HIGHEST, preferred_element_type=jnp.float32)
+
+
+def dot_nt(left, right):
+    return lax.dot_general(
+        left, right, (((1,), (1,)), ((), ())), precision=HIGHEST, preferred_element_type=jnp.float32
+    )
+
+
+def eliminate(matrix, target):
+    matrix = 0.5 * (matrix + matrix.T)
+    order = matrix.shape[0]
+    rows = lax.broadcasted_iota(jnp.int32, matrix.shape, 0)
+    for c in range(order):
+        column = jnp.broadcast_to(matrix[:, c : c + 1], matrix.shape)
+        scale = 1.0 / column[c : c + 1, :]
+        mrow = matrix[c : c + 1, :] * scale
+        trow = target[c : c + 1, :] * scale
+        here = rows == c
+        target = jnp.where(here, trow, target - column * trow)
+        if c < order - 1:
+            matrix = jnp.where(here, mrow, matrix - column * mrow)
+    return target
+
+
+def smooth(res, ngx, ngz):
+    lx, lz = len(res), len(res[0])
+    count, ny = res[0][0].shape
+    row = lax.broadcasted_iota(jnp.int32, (count, ny), 0)
+    lane = lax.broadcasted_iota(jnp.int32, (count, ny), 1)
+    even = lane % 2 == 0
+    edges = {
+        "xp": (row < ngz, ngz, 0),
+        "xn": (row >= count - ngz, count - ngz, 0),
+        "zp": (row % ngz == 0, 1, 0),
+        "zn": (row % ngz == ngz - 1, count - 1, 0),
+        "yp": (lane == 0, 1, 1),
+        "yn": (lane == ny - 1, ny - 1, 1),
+    }
+    zero = jnp.zeros((count, ny), jnp.float32)
+    memo = {}
+
+    def moved(value, kind):
+        if value is None:
+            return None
+        key = (kind, id(value))
+        if key not in memo:
+            edge, amount, axis = edges[kind]
+            memo[key] = (value, jnp.where(edge, zero, pltpu.roll(value, amount, axis)))
+        return memo[key][1]
+
+    def add(*values):
+        total = None
+        for value in values:
+            if value is not None:
+                total = value if total is None else total + value
+        return total
+
+    state = {(x, z): None for x in range(lx) for z in range(lz)}
+
+    def z_pair(x, z):
+        before = state[x, z - 1] if z > 0 else moved(state[x, lz - 1], "zp")
+        after = state[x, z + 1] if z < lz - 1 else moved(state[x, 0], "zn")
+        return add(before, after)
+
+    def neighbours(x, z):
+        def line(other):
+            return add(state[other, z], z_pair(other, z))
+
+        before = line(x - 1) if x > 0 else moved_line(lx - 1, z, "xp")
+        after = line(x + 1) if x < lx - 1 else moved_line(0, z, "xn")
+        return add(z_pair(x, z), before, after)
+
+    def moved_line(x, z, kind):
+        return moved(add(state[x, z], z_pair(x, z)), kind)
+
+    def y_pair(value):
+        return moved(value, "yp") + moved(value, "yn")
+
+    third = jnp.float32(1.0 / 26.0)
+    plan = [(0, 0, (0, 1)), (0, 1, (0, 1)), (1, 0, (0, 1)), (1, 1, (0, 1, 0)), (1, 0, (1, 0)), (0, 1, (1, 0)), (0, 0, (1, 0))]
+    for xp, zp, shades in plan:
+        fresh = {}
+        for x in range(xp, lx, 2):
+            for z in range(zp, lz, 2):
+                near = neighbours(x, z)
+                base = res[x][z] if near is None else res[x][z] + (near + y_pair(near))
+                value = state[x, z]
+                for shade in shades:
+                    total = base if value is None else base + y_pair(value)
+                    chosen = even if shade == 0 else jnp.logical_not(even)
+                    value = jnp.where(chosen, total * third, zero if value is None else value)
+                fresh[x, z] = value
+        state.update(fresh)
+    image = {}
+    for x in range(lx):
+        for z in range(lz):
+            box = add(state[x, z], neighbours(x, z))
+            image[x, z] = 27.0 * state[x, z] - (box + y_pair(box))
+    return state, image
+
+
+def kernel(
+    sizes, sol_in, res_in, dir_in, img_in, gram_in, sol_out, res_out, dir_out,
+    sol, res, prev, prev_img, gram, outs, land, done, back, part, parts,
+    local_sem, send_a, send_b, send_c, recv_sem,
+):
+    ngx, ngy, ngz, n, lx, lz, width = sizes
+    s = lx * lz
+    gx, gy, gz = lax.axis_index("gx"), lax.axis_index("gy"), lax.axis_index("gz")
+    column = gx * ngz + gz
+    place = gy * n + column
+    everyone = n * ngy
+
+    loads = [
+        pltpu.make_async_copy(a, b, local_sem.at[i])
+        for i, (a, b) in enumerate(((res_in, res), (gram_in, gram), (dir_in, prev), (img_in, prev_img), (sol_in, sol)))
+    ]
+    for load in loads:
+        load.start()
+
+    def peer(offset):
+        other = lax.rem(place + offset, everyone)
+        oy, oc = other // n, lax.rem(other, n)
+        return oc, {"gx": oc // ngz, "gy": oy, "gz": lax.rem(oc, ngz)}
+
+    barrier = pltpu.get_barrier_semaphore()
+    for offset in range(1, everyone):
+        pl.semaphore_signal(barrier, inc=1, device_id=peer(offset)[1], device_id_type=MESH)
+    loads[0].wait()
+    pl.semaphore_wait(barrier, everyone - 1)
+
+    sent = []
+    mine = land.at[pl.ds(place * s, s), :]
+    for offset in range(1, everyone):
+        oc, where = peer(offset)
+        copy = pltpu.make_async_remote_copy(
+            src_ref=res.at[pl.ds(oc * s, s), :], dst_ref=mine,
+            send_sem=send_a.at[offset], recv_sem=recv_sem.at[0], device_id=where, device_id_type=MESH,
+        )
+        copy.start()
+        sent.append(copy)
+    pltpu.make_async_copy(res.at[pl.ds(column * s, s), :], mine, recv_sem.at[0]).start()
+
+    def flat(ref, first, stride):
+        return jnp.concatenate([ref[pl.ds(first + i, n, stride=stride), :] for i in range(s)], axis=1)
+
+    for load in loads[1:4]:
+        load.wait()
+    eye = (lax.broadcasted_iota(jnp.int32, (n, n), 0) == lax.broadcasted_iota(jnp.int32, (n, n), 1)).astype(jnp.float32)
+    inverse = eliminate(gram[...], eye)
+    p, q, r = flat(prev, 0, s), flat(prev_img, 0, s), flat(res, 0, s)
+    gram_pq = dot_nt(p, q)
+
+    pltpu.make_async_copy(land, land, recv_sem.at[0]).wait()
+    field = [
+        [
+            jnp.concatenate(
+                [land[pl.ds(y * n * s + x * lz + z, n, stride=s), :] for y in range(ngy)], axis=1
+            )
+            for z in range(lz)
+        ]
+        for x in range(lx)
+    ]
+    state, image = smooth(field, ngx, ngz)
+    for x in range(lx):
+        for z in range(lz):
+            for y in range(ngy):
+                first = y * n * 2 * s + x * lz + z
+                cut = slice(y * width, (y + 1) * width)
+                done[pl.ds(first, n, stride=2 * s), :] = state[x, z][:, cut]
+                done[pl.ds(first + s, n, stride=2 * s), :] = image[x, z][:, cut]
+    mine = back.at[pl.ds(column * 2 * s, 2 * s), :]
+    for offset in range(1, n):
+        oc = lax.rem(column + offset, n)
+        copy = pltpu.make_async_remote_copy(
+            src_ref=done.at[pl.ds((gy * n + oc) * 2 * s, 2 * s), :], dst_ref=mine,
+            send_sem=send_b.at[offset], recv_sem=recv_sem.at[1],
+            device_id={"gx": oc // ngz, "gy": gy, "gz": lax.rem(oc, ngz)}, device_id_type=MESH,
+        )
+        copy.start()
+        sent.append(copy)
+    pltpu.make_async_copy(done.at[pl.ds(place * 2 * s, 2 * s), :], mine, recv_sem.at[1]).start()
+    pltpu.make_async_copy(back, back, recv_sem.at[1]).wait()
+
+    zf, wf = flat(back, 0, 2 * s), flat(back, s, 2 * s)
+    sums = dot_nt(zf, jnp.concatenate([r, wf, q], axis=0))
+    sums = jnp.concatenate([sums, gram_pq], axis=1)
+    half = n // 2
+    part[...] = jnp.concatenate([sums[:half], sums[half:]], axis=1)
+    mine = parts.at[pl.ds(place * half, half), :]
+    for offset in range(1, everyone):
+        copy = pltpu.make_async_remote_copy(
+            src_ref=part, dst_ref=mine,
+            send_sem=send_c.at[offset], recv_sem=recv_sem.at[2], device_id=peer(offset)[1], device_id_type=MESH,
+        )
+        copy.start()
+        sent.append(copy)
+    pltpu.make_async_copy(part, mine, recv_sem.at[2]).start()
+    pltpu.make_async_copy(parts, parts, recv_sem.at[2]).wait()
+
+    level = [parts[i * half : (i + 1) * half, :] for i in range(everyone)]
+    while len(level) > 1:
+        level = [sum(level[i + 1 : i + 2], level[i]) for i in range(0, len(level), 2)]
+    total = level[0]
+    total = jnp.concatenate([total[:, : 4 * n], total[:, 4 * n :]], axis=0)
+    gram_zr, gram_zw, gram_zq, gram_pq = (total[:, i * n : (i + 1) * n] for i in range(4))
+
+    beta = dot(inverse, gram_zr)
+    cross = dot(jnp.concatenate([gram_zq, gram_pq], axis=0), beta)
+    beta_t = beta.T
+    curvature = gram_zw + cross[:n] + cross[:n].T + dot(beta_t, cross[n:])
+    mixed = dot(beta_t, jnp.concatenate([p, q], axis=1))
+    direction = zf + mixed[:, : s * width]
+    image_new = wf + mixed[:, s * width :]
+    alpha = eliminate(curvature, gram_zr)
+    step = dot(alpha.T, jnp.concatenate([direction, image_new], axis=1))
+    loads[4].wait()
+    for i in range(s):
+        rows = pl.ds(i, n, stride=s)
+        cut = slice(i * width, (i + 1) * width)
+        outs[2, rows, :] = direction[:, cut]
+        outs[0, rows, :] = sol[rows, :] + step[:, cut]
+        outs[1, rows, :] = res[rows, :] - step[:, s * width + i * width : s * width + (i + 1) * width]
+    stores = [
+        pltpu.make_async_copy(outs.at[i], out, local_sem.at[i]) for i, out in enumerate((sol_out, res_out, dir_out))
+    ]
+    for store in stores:
+        store.start()
+    for copy in sent:
+        copy.wait_send()
+    for store in stores:
+        store.wait()
+
+
+def whole_body(sizes, solution, residual, direction_prev, image_prev, gram_prev):
+    ngx, ngy, ngz, n, lx, lz, width = sizes
+    s, everyone = lx * lz, n * ngy
+    rows = n * s
+    shape = residual.shape
+    field = jax.ShapeDtypeStruct((rows, width), jnp.float32)
+    outs = pl.pallas_call(
+        functools.partial(kernel, sizes),
+        out_shape=(field, field, field),
+        in_specs=[pl.BlockSpec(memory_space=pl.ANY)] * 5,
+        out_specs=[pl.BlockSpec(memory_space=pl.ANY)] * 3,
+        scratch_shapes=[pltpu.VMEM((rows, width), jnp.float32)] * 4
+        + [
+            pltpu.VMEM((n, n), jnp.float32),
+            pltpu.VMEM((3, rows, width), jnp.float32),
+            pltpu.VMEM((everyone * s, width), jnp.float32),
+            pltpu.VMEM((everyone * 2 * s, width), jnp.float32),
+            pltpu.VMEM((n * 2 * s, width), jnp.float32),
+            pltpu.VMEM((n // 2, 8 * n), jnp.float32),
+            pltpu.VMEM((everyone * (n // 2), 8 * n), jnp.float32),
+            pltpu.SemaphoreType.DMA((5,)),
+            pltpu.SemaphoreType.DMA((everyone,)),
+            pltpu.SemaphoreType.DMA((n,)),
+            pltpu.SemaphoreType.DMA((everyone,)),
+            pltpu.SemaphoreType.DMA((3,)),
+        ],
+        compiler_params=pltpu.CompilerParams(collective_id=0, has_side_effects=True),
+    )(*(a.reshape(rows, width) for a in (solution, residual, direction_prev, image_prev)), gram_prev)
+    return tuple(a.reshape(shape) for a in outs)
+
+
+def pick_body(mesh, solution, residual, direction_prev, image_prev, gram_prev):
+    ngx, ngy, ngz = (mesh.shape[axis] for axis in ("gx", "gy", "gz"))
+    n, lx, lz, width = residual.shape
+    fits = n == ngx * ngz and lx % 2 == 0 and lz % 2 == 0 and (lx * lz) % 8 == 0
+    fits = fits and width % 128 == 0 and n % 16 == 0
+    args = (solution, residual, direction_prev, image_prev, gram_prev)
+    if fits:
+        return whole_body((ngx, ngy, ngz, n, lx, lz, width), *args)
+    return body(*args)
+
+
 def solution(mesh):
     in_specs = (
         P(None, "gx", "gz", "gy"),
@@ -104,4 +390,4 @@
         P(),
     )
     out_specs = (P(None, "gx", "gz", "gy"), P(None, "gx", "gz", "gy"), P(None, "gx", "gz", "gy"))
-    return jax.shard_map(body, mesh=mesh, in_specs=in_specs, out_specs=out_specs, check_vma=False)
+    return jax.shard_map(functools.partial(pick_body, mesh), mesh=mesh, in_specs=in_specs, out_specs=out_specs, check_vma=False)

time: 498 us -> 32 us (0.06)
  starting transfers between devices: 267 us -> 0 us
  waiting for transfers between devices: 71.8 us -> 0 us
  other arithmetic: 62.7 us -> 0 us
  blocking collectives: 47.6 us -> 0 us
  local copies, waits for them, and re-layouts: 32.4 us -> 3 us
  Pallas kernels: 0 us -> 28.1 us
  between operations: 11.3 us -> 0.65 us
    ppermute x90 -> x0, starting transfers between devices: 267 us -> none  [the longest x45 209 us: with_halo(): before = lax.ppermute(last, axis, up)]
    ppermute x90 -> x0, waiting for transfers between devices: 71.8 us -> none  [the longest x45 54.6 us: with_halo(): before = lax.ppermute(last, axis, up)]
    psum x1 -> x0, blocking collectives: 47.6 us -> none  [body(): lax.psum((sums[0], sums[1], sums[2], sums[3], sums[4]), ('gx', 'gy', 'gz'))]
    div x86 -> x0, other arithmetic: 42.1 us -> none  [the longest x30 20.1 us: spd_solve(): answer = answer.at[row].set(value / lower[row, row])]
    pallas_call x0 -> x1, Pallas kernels: none -> 28.1 us  [whole_body(): pl.pallas_call(functools.partial(kernel, sizes), out_shape=(field, field,...]
    slice x94 -> x0, local copies, waits for them, and re-layouts: 16.9 us -> none  [the longest x30 6.08 us: spd_solve(): lower[row + 1:, row][:, None] * answer[row + 1:]]
    scatter x92 -> x0, local copies, waits for them, and re-layouts: 9.63 us -> none  [the longest x30 7.29 us: spd_solve(): lower = lower.at[col:, col].set(column / pivot)]
    reduce_sum x82 -> x0, other arithmetic: 7.98 us -> none  [the longest x26 3.01 us: spd_solve(): jnp.sum(lower[col:, :col] * lower[col, :col][None, :], axis=1)]
  transfers between devices with their start and end apart: 90 -> 0, of which waited for: 71 -> 0; matrix products, arithmetic and copies ran while one was open for 4% -> 0% of each run, Pallas kernels for 0% -> 0%
where the time goes in v1:
time: 32 us; the launch traced here: 31.8 us
  Pallas kernels  28.1 us (88%)
  local copies, waits for them, and re-layouts  3 us (9%)
  between operations  0.65 us (2%)
    pallas_call x1, Pallas kernels, whole_body(): pl.pallas_call(functools.partial(kernel, sizes), out_shape=(field, field,...  28.1 us
    unnamed x7, local copies, waits for them, and re-layouts  3 us

profile of v1, /device:TPU:0, one launch (start us, length us, event | category | flops | bytes accessed | tf_op | source)
XLA Modules:
  0.0 31.8 jit_solution(8919683748971556995)
XLA Ops:
  0.6 28.1 %shard_map.76 = (f32[128,128]{1,0:T(8,128)}, f32[128,128]{1,0:T(8,128)}, f32[128,128]{1,0:T(8,128)}) custom-call(f32[128,128]{1,0:T(8,128)} %bitcast.10, f32[128,128]{1,0:T(8,128)} %bitcast.11, f32[128,128]{1,0:T(8,128)} %bitcast.12, f32[128,128]{1,0:T(8,128)} %bitcast.13, f32[16,16]{1,0:T(8,128)} %gram_in.1), custom_call_target="tpu_custom_call" | custom-call | tf_op jit(solution)/shard_map/pallas_call | solution.py:348
  28.8 0.0 copy-start.1
  28.8 1.5 %copy.11 = f32[16,2,4,128]{3,2,1,0:T(4,128)} copy(f32[16,2,4,128]{3,2,1,0:T(4,128)} %bitcast.9) | data formatting | bytes 131072
  30.3 0.0 copy-done.1
  30.3 0.0 copy-start
  30.3 0.6 %copy.12 = f32[16,2,4,128]{3,2,1,0:T(4,128)} copy(f32[16,2,4,128]{3,2,1,0:T(4,128)S(1)} %bitcast.8) | data formatting | bytes 131072
  30.9 0.2 copy-done
  31.1 0.6 %copy.13 = f32[16,2,4,128]{3,2,1,0:T(4,128)} copy(f32[16,2,4,128]{3,2,1,0:T(4,128)S(1)} %bitcast.7) | data formatting | bytes 131072
Async XLA Ops:
  28.8 1.5 %copy-start.1 = (f32[128,128]{1,0:T(8,128)S(1)}, f32[128,128]{1,0:T(8,128)}, u32[]{:S(2)}) copy-start(f32[128,128]{1,0:T(8,128)} %get-tuple-element.7) | copy-start | bytes 196612
  30.3 0.9 %copy-start = (f32[128,128]{1,0:T(8,128)S(1)}, f32[128,128]{1,0:T(8,128)}, u32[]{:S(2)}) copy-start(f32[128,128]{1,0:T(8,128)} %get-tuple-element.8) | copy-start | bytes 196612

commit v2 on v1

--- a/solution.py
+++ b/solution.py
@@ -207,8 +207,8 @@
 
 
 def kernel(
-    sizes, sol_in, res_in, dir_in, img_in, gram_in, sol_out, res_out, dir_out,
-    sol, res, prev, prev_img, gram, outs, land, done, back, part, parts,
+    sizes, res_in, dir_in, img_in, gram_in, back_out, small_out,
+    res, prev, prev_img, gram, small, land, done, back, part, parts,
     local_sem, send_a, send_b, send_c, recv_sem,
 ):
     ngx, ngy, ngz, n, lx, lz, width = sizes
@@ -220,15 +220,20 @@
 
     loads = [
         pltpu.make_async_copy(a, b, local_sem.at[i])
-        for i, (a, b) in enumerate(((res_in, res), (gram_in, gram), (dir_in, prev), (img_in, prev_img), (sol_in, sol)))
+        for i, (a, b) in enumerate(((res_in, res), (gram_in, gram), (dir_in, prev), (img_in, prev_img)))
     ]
     for load in loads:
         load.start()
 
+    ways = sorted(
+        ((dx, dy, dz) for dx in range(ngx) for dy in range(ngy) for dz in range(ngz)),
+        key=lambda way: (-min(way[2], ngz - way[2]), -min(way[0], ngx - way[0]), -way[1]),
+    )[:-1]
+
     def peer(offset):
-        other = lax.rem(place + offset, everyone)
-        oy, oc = other // n, lax.rem(other, n)
-        return oc, {"gx": oc // ngz, "gy": oy, "gz": lax.rem(oc, ngz)}
+        dx, dy, dz = ways[offset - 1]
+        ox, oy, oz = lax.rem(gx + dx, ngx), lax.rem(gy + dy, ngy), lax.rem(gz + dz, ngz)
+        return ox * ngz + oz, {"gx": ox, "gy": oy, "gz": oz}
 
     barrier = pltpu.get_barrier_semaphore()
     for offset in range(1, everyone):
@@ -277,8 +282,8 @@
                 done[pl.ds(first, n, stride=2 * s), :] = state[x, z][:, cut]
                 done[pl.ds(first + s, n, stride=2 * s), :] = image[x, z][:, cut]
     mine = back.at[pl.ds(column * 2 * s, 2 * s), :]
-    for offset in range(1, n):
-        oc = lax.rem(column + offset, n)
+    for offset, (dx, _, dz) in enumerate(way for way in ways if way[1] == 0):
+        oc = lax.rem(gx + dx, ngx) * ngz + lax.rem(gz + dz, ngz)
         copy = pltpu.make_async_remote_copy(
             src_ref=done.at[pl.ds((gy * n + oc) * 2 * s, 2 * s), :], dst_ref=mine,
             send_sem=send_b.at[offset], recv_sem=recv_sem.at[1],
@@ -292,6 +297,8 @@
     zf, wf = flat(back, 0, 2 * s), flat(back, s, 2 * s)
     sums = dot_nt(zf, jnp.concatenate([r, wf, q], axis=0))
     sums = jnp.concatenate([sums, gram_pq], axis=1)
+    keep = pltpu.make_async_copy(back, back_out, local_sem.at[0])
+    keep.start()
     half = n // 2
     part[...] = jnp.concatenate([sums[:half], sums[half:]], axis=1)
     mine = parts.at[pl.ds(place * half, half), :]
@@ -309,6 +316,38 @@
     while len(level) > 1:
         level = [sum(level[i + 1 : i + 2], level[i]) for i in range(0, len(level), 2)]
     total = level[0]
+    small[:half, :] = total
+    small[half:, :] = jnp.concatenate([inverse[:half], inverse[half:], jnp.zeros((half, 6 * n), jnp.float32)], axis=1)
+    store = pltpu.make_async_copy(small, small_out, local_sem.at[1])
+    store.start()
+    for copy in sent:
+        copy.wait_send()
+    keep.wait()
+    store.wait()
+
+
+def finish(
+    sizes, sol_in, res_in, dir_in, img_in, back_in, small_in, sol_out, res_out, dir_out,
+    sol, res, prev, prev_img, back, small, outs, local_sem,
+):
+    ngx, ngy, ngz, n, lx, lz, width = sizes
+    s, half = lx * lz, n // 2
+    loads = [
+        pltpu.make_async_copy(a, b, local_sem.at[i])
+        for i, (a, b) in enumerate(
+            ((small_in, small), (dir_in, prev), (img_in, prev_img), (back_in, back), (sol_in, sol), (res_in, res))
+        )
+    ]
+    for load in loads:
+        load.start()
+
+    def flat(ref, first, stride):
+        return jnp.concatenate([ref[pl.ds(first + i, n, stride=stride), :] for i in range(s)], axis=1)
+
+    loads[0].wait()
+    total = small[:half, :]
+    inverse = small[half:, :]
+    inverse = jnp.concatenate([inverse[:, :n], inverse[:, n : 2 * n]], axis=0)
     total = jnp.concatenate([total[:, : 4 * n], total[:, 4 * n :]], axis=0)
     gram_zr, gram_zw, gram_zq, gram_pq = (total[:, i * n : (i + 1) * n] for i in range(4))
 
@@ -316,12 +355,16 @@
     cross = dot(jnp.concatenate([gram_zq, gram_pq], axis=0), beta)
     beta_t = beta.T
     curvature = gram_zw + cross[:n] + cross[:n].T + dot(beta_t, cross[n:])
+    for load in loads[1:4]:
+        load.wait()
+    p, q, zf, wf = flat(prev, 0, s), flat(prev_img, 0, s), flat(back, 0, 2 * s), flat(back, s, 2 * s)
     mixed = dot(beta_t, jnp.concatenate([p, q], axis=1))
     direction = zf + mixed[:, : s * width]
     image_new = wf + mixed[:, s * width :]
     alpha = eliminate(curvature, gram_zr)
     step = dot(alpha.T, jnp.concatenate([direction, image_new], axis=1))
     loads[4].wait()
+    loads[5].wait()
     for i in range(s):
         rows = pl.ds(i, n, stride=s)
         cut = slice(i * width, (i + 1) * width)
@@ -333,8 +376,6 @@
     ]
     for store in stores:
         store.start()
-    for copy in sent:
-        copy.wait_send()
     for store in stores:
         store.wait()
 
@@ -345,28 +386,50 @@
     rows = n * s
     shape = residual.shape
     field = jax.ShapeDtypeStruct((rows, width), jnp.float32)
-    outs = pl.pallas_call(
+    anywhere = pl.BlockSpec(memory_space=pl.ANY)
+    block = pltpu.VMEM((rows, width), jnp.float32)
+    packed = pltpu.VMEM((n, 8 * n), jnp.float32)
+    solution, residual, direction_prev, image_prev = (
+        a.reshape(rows, width) for a in (solution, residual, direction_prev, image_prev)
+    )
+    back, small = pl.pallas_call(
         functools.partial(kernel, sizes),
-        out_shape=(field, field, field),
-        in_specs=[pl.BlockSpec(memory_space=pl.ANY)] * 5,
-        out_specs=[pl.BlockSpec(memory_space=pl.ANY)] * 3,
-        scratch_shapes=[pltpu.VMEM((rows, width), jnp.float32)] * 4
-        + [
+        out_shape=(
+            jax.ShapeDtypeStruct((2 * rows, width), jnp.float32),
+            jax.ShapeDtypeStruct((n, 8 * n), jnp.float32),
+        ),
+        in_specs=[anywhere] * 4,
+        out_specs=[anywhere] * 2,
+        scratch_shapes=[
+            block, block, block,
             pltpu.VMEM((n, n), jnp.float32),
-            pltpu.VMEM((3, rows, width), jnp.float32),
+            packed,
             pltpu.VMEM((everyone * s, width), jnp.float32),
             pltpu.VMEM((everyone * 2 * s, width), jnp.float32),
-            pltpu.VMEM((n * 2 * s, width), jnp.float32),
+            pltpu.VMEM((2 * rows, width), jnp.float32),
             pltpu.VMEM((n // 2, 8 * n), jnp.float32),
             pltpu.VMEM((everyone * (n // 2), 8 * n), jnp.float32),
-            pltpu.SemaphoreType.DMA((5,)),
+            pltpu.SemaphoreType.DMA((4,)),
             pltpu.SemaphoreType.DMA((everyone,)),
             pltpu.SemaphoreType.DMA((n,)),
             pltpu.SemaphoreType.DMA((everyone,)),
             pltpu.SemaphoreType.DMA((3,)),
         ],
         compiler_params=pltpu.CompilerParams(collective_id=0, has_side_effects=True),
-    )(*(a.reshape(rows, width) for a in (solution, residual, direction_prev, image_prev)), gram_prev)
+    )(residual, direction_prev, image_prev, gram_prev)
+    outs = pl.pallas_call(
+        functools.partial(finish, sizes),
+        out_shape=(field, field, field),
+        in_specs=[anywhere] * 6,
+        out_specs=[anywhere] * 3,
+        scratch_shapes=[
+            block, block, block, block,
+            pltpu.VMEM((2 * rows, width), jnp.float32),
+            packed,
+            pltpu.VMEM((3, rows, width), jnp.float32),
+            pltpu.SemaphoreType.DMA((6,)),
+        ],
+    )(solution, residual, direction_prev, image_prev, back, small)
     return tuple(a.reshape(shape) for a in outs)
 
 

time: 32 us -> 29.5 us (0.922)
  local copies, waits for them, and re-layouts: 3 us -> 0 us
  Pallas kernels: 28.1 us -> 28.6 us
    unnamed x7 -> x0, local copies, waits for them, and re-layouts: 3 us -> none
    pallas_call x1 -> x2, Pallas kernels: 28.1 us -> 28.6 us  [the longest x1 24.7 us: whole_body(): pl.pallas_call(functools.partial(kernel, sizes), out_shape=(jax.ShapeDtyp...]
where the time goes in v2:
time: 29.5 us; the launch traced here: 29.3 us
  Pallas kernels  28.6 us (97%)
  between operations  0.64 us (2%)
    pallas_call x1, Pallas kernels, whole_body(): pl.pallas_call(functools.partial(kernel, sizes), out_shape=(jax.ShapeDtyp...  24.7 us
    pallas_call x1, Pallas kernels, whole_body(): pl.pallas_call(functools.partial(finish, sizes), out_shape=(field, field,...  3.92 us

profile of v2, /device:TPU:0, one launch (start us, length us, event | category | flops | bytes accessed | tf_op | source)
XLA Modules:
  0.0 29.3 jit_solution(5004499445384027144)
XLA Ops:
  0.6 24.7 %shard_map.76 = (f32[256,128]{1,0:T(8,128)}, f32[16,128]{1,0:T(8,128)}) custom-call(f32[128,128]{1,0:T(8,128)} %bitcast.7, f32[128,128]{1,0:T(8,128)} %bitcast.9, f32[128,128]{1,0:T(8,128)} %bitcast.11, f32[16,16]{1,0:T(8,128)} %gram_in.1), custom_call_target="tpu_custom_call" | custom-call | tf_op jit(solution)/shard_map/pallas_call | solution.py:395
  25.3 3.9 %shard_map.77 = (f32[128,128]{1,0:T(8,128)}, f32[128,128]{1,0:T(8,128)}, f32[128,128]{1,0:T(8,128)}) custom-call(f32[128,128]{1,0:T(8,128)} %bitcast.13, f32[128,128]{1,0:T(8,128)} %bitcast.8, f32[128,128]{1,0:T(8,128)} %bitcast.10, f32[128,128]{1,0:T(8,128)} %bitcast.12, f32[256,128]{1,0:T(8,128)} %get-tuple-element.8.back_in, ...), custom_call_target="tpu_custom_call" | custom-call | tf_op jit(solution)/shard_map/pallas_call | solution.py:420

commit v3 on v2

--- a/solution.py
+++ b/solution.py
@@ -129,7 +129,7 @@
     return target
 
 
-def smooth(res, ngx, ngz):
+def smooth(res, ngx, ngz, gy, width):
     lx, lz = len(res), len(res[0])
     count, ny = res[0][0].shape
     row = lax.broadcasted_iota(jnp.int32, (count, ny), 0)
@@ -140,8 +140,8 @@
         "xn": (row >= count - ngz, count - ngz, 0),
         "zp": (row % ngz == 0, 1, 0),
         "zn": (row % ngz == ngz - 1, count - 1, 0),
-        "yp": (lane == 0, 1, 1),
-        "yn": (lane == ny - 1, ny - 1, 1),
+        "yp": (lane == jnp.where(gy == 0, 0, -1), 1, 1),
+        "yn": (lane == jnp.where(gy == 0, -1, width - 1), ny - 1, 1),
     }
     zero = jnp.zeros((count, ny), jnp.float32)
     memo = {}
@@ -208,7 +208,7 @@
 
 def kernel(
     sizes, res_in, dir_in, img_in, gram_in, back_out, small_out,
-    res, prev, prev_img, gram, small, land, done, back, part, parts,
+    res, prev, prev_img, gram, small, land, strip, halo, done, back, part, parts,
     local_sem, send_a, send_b, send_c, recv_sem,
 ):
     ngx, ngy, ngz, n, lx, lz, width = sizes
@@ -239,15 +239,27 @@
     for offset in range(1, everyone):
         pl.semaphore_signal(barrier, inc=1, device_id=peer(offset)[1], device_id_type=MESH)
     loads[0].wait()
+    depth = width // s
+    lanes = lax.broadcasted_iota(jnp.int32, (n, width), 1)
+    packed = jnp.zeros((n, width), jnp.float32)
+    for i in range(s):
+        line = res[pl.ds(i, n, stride=s), :]
+        line = pltpu.roll(line, lax.rem(i * depth + jnp.where(gy == 0, depth, 0), width), 1)
+        packed = jnp.where(lanes // depth == i, line, packed)
+    for i in range(n):
+        strip[i] = packed[i : i + 1, :]
     pl.semaphore_wait(barrier, everyone - 1)
 
     sent = []
-    mine = land.at[pl.ds(place * s, s), :]
+    mine = land.at[pl.ds(column * s, s), :]
     for offset in range(1, everyone):
         oc, where = peer(offset)
+        near = ways[offset - 1][1] == 0
         copy = pltpu.make_async_remote_copy(
-            src_ref=res.at[pl.ds(oc * s, s), :], dst_ref=mine,
-            send_sem=send_a.at[offset], recv_sem=recv_sem.at[0], device_id=where, device_id_type=MESH,
+            src_ref=res.at[pl.ds(oc * s, s), :] if near else strip.at[oc],
+            dst_ref=mine if near else halo.at[column],
+            send_sem=send_a.at[offset], recv_sem=recv_sem.at[0 if near else 3],
+            device_id=where, device_id_type=MESH,
         )
         copy.start()
         sent.append(copy)
@@ -264,34 +276,33 @@
     gram_pq = dot_nt(p, q)
 
     pltpu.make_async_copy(land, land, recv_sem.at[0]).wait()
-    field = [
-        [
-            jnp.concatenate(
-                [land[pl.ds(y * n * s + x * lz + z, n, stride=s), :] for y in range(ngy)], axis=1
-            )
-            for z in range(lz)
-        ]
-        for x in range(lx)
-    ]
-    state, image = smooth(field, ngx, ngz)
+    pltpu.make_async_copy(halo, halo, recv_sem.at[3]).wait()
+    rows = jnp.concatenate([halo[i] for i in range(n)], axis=0)
+    outside = jnp.where(gy == 0, 0, s - 1)
+
+    def extended(i):
+        shift = lax.rem((2 * s - i + outside) * depth, width)
+        beside = jnp.where(lanes // depth == outside, pltpu.roll(rows, shift, 1), 0.0)
+        return jnp.concatenate([land[pl.ds(i, n, stride=s), :], beside], axis=1)
+
+    field = [[extended(x * lz + z) for z in range(lz)] for x in range(lx)]
+    state, image = smooth(field, ngx, ngz, gy, width)
     for x in range(lx):
         for z in range(lz):
-            for y in range(ngy):
-                first = y * n * 2 * s + x * lz + z
-                cut = slice(y * width, (y + 1) * width)
-                done[pl.ds(first, n, stride=2 * s), :] = state[x, z][:, cut]
-                done[pl.ds(first + s, n, stride=2 * s), :] = image[x, z][:, cut]
+            first = x * lz + z
+            done[pl.ds(first, n, stride=2 * s), :] = state[x, z][:, :width]
+            done[pl.ds(first + s, n, stride=2 * s), :] = image[x, z][:, :width]
     mine = back.at[pl.ds(column * 2 * s, 2 * s), :]
     for offset, (dx, _, dz) in enumerate(way for way in ways if way[1] == 0):
         oc = lax.rem(gx + dx, ngx) * ngz + lax.rem(gz + dz, ngz)
         copy = pltpu.make_async_remote_copy(
-            src_ref=done.at[pl.ds((gy * n + oc) * 2 * s, 2 * s), :], dst_ref=mine,
+            src_ref=done.at[pl.ds(oc * 2 * s, 2 * s), :], dst_ref=mine,
             send_sem=send_b.at[offset], recv_sem=recv_sem.at[1],
             device_id={"gx": oc // ngz, "gy": gy, "gz": lax.rem(oc, ngz)}, device_id_type=MESH,
         )
         copy.start()
         sent.append(copy)
-    pltpu.make_async_copy(done.at[pl.ds(place * 2 * s, 2 * s), :], mine, recv_sem.at[1]).start()
+    pltpu.make_async_copy(done.at[pl.ds(column * 2 * s, 2 * s), :], mine, recv_sem.at[1]).start()
     pltpu.make_async_copy(back, back, recv_sem.at[1]).wait()
 
     zf, wf = flat(back, 0, 2 * s), flat(back, s, 2 * s)
@@ -404,8 +415,10 @@
             block, block, block,
             pltpu.VMEM((n, n), jnp.float32),
             packed,
-            pltpu.VMEM((everyone * s, width), jnp.float32),
-            pltpu.VMEM((everyone * 2 * s, width), jnp.float32),
+            pltpu.VMEM((rows, width), jnp.float32),
+            pltpu.VMEM((n, 1, width), jnp.float32),
+            pltpu.VMEM((n, 1, width), jnp.float32),
+            pltpu.VMEM((2 * rows, width), jnp.float32),
             pltpu.VMEM((2 * rows, width), jnp.float32),
             pltpu.VMEM((n // 2, 8 * n), jnp.float32),
             pltpu.VMEM((everyone * (n // 2), 8 * n), jnp.float32),
@@ -413,7 +426,7 @@
             pltpu.SemaphoreType.DMA((everyone,)),
             pltpu.SemaphoreType.DMA((n,)),
             pltpu.SemaphoreType.DMA((everyone,)),
-            pltpu.SemaphoreType.DMA((3,)),
+            pltpu.SemaphoreType.DMA((4,)),
         ],
         compiler_params=pltpu.CompilerParams(collective_id=0, has_side_effects=True),
     )(residual, direction_prev, image_prev, gram_prev)
@@ -437,7 +450,7 @@
     ngx, ngy, ngz = (mesh.shape[axis] for axis in ("gx", "gy", "gz"))
     n, lx, lz, width = residual.shape
     fits = n == ngx * ngz and lx % 2 == 0 and lz % 2 == 0 and (lx * lz) % 8 == 0
-    fits = fits and width % 128 == 0 and n % 16 == 0
+    fits = fits and width % 128 == 0 and n % 16 == 0 and ngy == 2 and width % (lx * lz) == 0 and width // (lx * lz) >= 15
     args = (solution, residual, direction_prev, image_prev, gram_prev)
     if fits:
         return whole_body((ngx, ngy, ngz, n, lx, lz, width), *args)

time: 29.5 us -> 28.8 us (0.976)
  Pallas kernels: 28.6 us -> 27.9 us
    pallas_call x1, Pallas kernels: 24.7 us -> 24 us  [whole_body(): pl.pallas_call(functools.partial(kernel, sizes), out_shape=(jax.ShapeDtyp...]
where the time goes in v3:
time: 28.8 us; the launch traced here: 28.6 us
  Pallas kernels  27.9 us (97%)
  between operations  0.64 us (2%)
    pallas_call x1, Pallas kernels, whole_body(): pl.pallas_call(functools.partial(kernel, sizes), out_shape=(jax.ShapeDtyp...  24 us
    pallas_call x1, Pallas kernels, whole_body(): pl.pallas_call(functools.partial(finish, sizes), out_shape=(field, field,...  3.92 us

profile of v3, /device:TPU:0, one launch (start us, length us, event | category | flops | bytes accessed | tf_op | source)
XLA Modules:
  0.0 28.6 jit_solution(16139167945774520036)
XLA Ops:
  0.6 24.0 %shard_map.76 = (f32[256,128]{1,0:T(8,128)}, f32[16,128]{1,0:T(8,128)}) custom-call(f32[128,128]{1,0:T(8,128)} %bitcast.7, f32[128,128]{1,0:T(8,128)} %bitcast.9, f32[128,128]{1,0:T(8,128)} %bitcast.11, f32[16,16]{1,0:T(8,128)} %gram_in.1), custom_call_target="tpu_custom_call" | custom-call | tf_op jit(solution)/shard_map/pallas_call | solution.py:406
  24.7 3.9 %shard_map.77 = (f32[128,128]{1,0:T(8,128)}, f32[128,128]{1,0:T(8,128)}, f32[128,128]{1,0:T(8,128)}) custom-call(f32[128,128]{1,0:T(8,128)} %bitcast.13, f32[128,128]{1,0:T(8,128)} %bitcast.8, f32[128,128]{1,0:T(8,128)} %bitcast.10, f32[128,128]{1,0:T(8,128)} %bitcast.12, f32[256,128]{1,0:T(8,128)} %get-tuple-element.8.back_in, ...), custom_call_target="tpu_custom_call" | custom-call | tf_op jit(solution)/shard_map/pallas_call | solution.py:433

commit v4 on v3

--- a/solution.py
+++ b/solution.py
@@ -114,19 +114,14 @@
 
 
 def eliminate(matrix, target):
-    matrix = 0.5 * (matrix + matrix.T)
     order = matrix.shape[0]
-    rows = lax.broadcasted_iota(jnp.int32, matrix.shape, 0)
+    both = jnp.concatenate([0.5 * (matrix + matrix.T), target], axis=1)
+    rows = lax.broadcasted_iota(jnp.int32, both.shape, 0)
     for c in range(order):
-        column = jnp.broadcast_to(matrix[:, c : c + 1], matrix.shape)
-        scale = 1.0 / column[c : c + 1, :]
-        mrow = matrix[c : c + 1, :] * scale
-        trow = target[c : c + 1, :] * scale
-        here = rows == c
-        target = jnp.where(here, trow, target - column * trow)
-        if c < order - 1:
-            matrix = jnp.where(here, mrow, matrix - column * mrow)
-    return target
+        column = jnp.broadcast_to(both[:, c : c + 1], both.shape)
+        line = both[c : c + 1, :] / column[c : c + 1, :]
+        both = jnp.where(rows == c, line, both - column * line)
+    return both[:, order:]
 
 
 def smooth(res, ngx, ngz, gy, width):

time: 28.8 us -> 29 us (level)
  Pallas kernels: 27.9 us -> 28.2 us
where the time goes in v4:
time: 29 us; the launch traced here: 28.8 us
  Pallas kernels  28.2 us (97%)
  between operations  0.64 us (2%)
    pallas_call x1, Pallas kernels, whole_body(): pl.pallas_call(functools.partial(kernel, sizes), out_shape=(jax.ShapeDtyp...  24.1 us
    pallas_call x1, Pallas kernels, whole_body(): pl.pallas_call(functools.partial(finish, sizes), out_shape=(field, field,...  4.1 us

profile of v4, /device:TPU:0, one launch (start us, length us, event | category | flops | bytes accessed | tf_op | source)
XLA Modules:
  0.0 28.8 jit_solution(18130265849364545774)
XLA Ops:
  0.6 24.1 %shard_map.76 = (f32[256,128]{1,0:T(8,128)}, f32[16,128]{1,0:T(8,128)}) custom-call(f32[128,128]{1,0:T(8,128)} %bitcast.7, f32[128,128]{1,0:T(8,128)} %bitcast.9, f32[128,128]{1,0:T(8,128)} %bitcast.11, f32[16,16]{1,0:T(8,128)} %gram_in.1), custom_call_target="tpu_custom_call" | custom-call | tf_op jit(solution)/shard_map/pallas_call | solution.py:401
  24.7 4.1 %shard_map.77 = (f32[128,128]{1,0:T(8,128)}, f32[128,128]{1,0:T(8,128)}, f32[128,128]{1,0:T(8,128)}) custom-call(f32[128,128]{1,0:T(8,128)} %bitcast.13, f32[128,128]{1,0:T(8,128)} %bitcast.8, f32[128,128]{1,0:T(8,128)} %bitcast.10, f32[128,128]{1,0:T(8,128)} %bitcast.12, f32[256,128]{1,0:T(8,128)} %get-tuple-element.8.back_in, ...), custom_call_target="tpu_custom_call" | custom-call | tf_op jit(solution)/shard_map/pallas_call | solution.py:428
